TPU v7x, 128 devices: a whole 4x4x4 slice. The times are simulated.
128 devices in a mesh: row: 8 (over x, core), col: 16 (over z, y).
Axes of the slice: x: 4, y: 4, z: 4, core: 2. Of those that a mesh axis runs over, the one named last changes fastest.
Arguments:
- tail_vectors: float32 [64512, 4096], P('row', 'col'), may hold values from -6 to 6
- lower_panel: float32 [64512, 1024], P(('row', 'col')), may hold values from -0.0234375 to 0.0234375
- window_rhs: float32 [1024, 4096], P('row', 'col'), may hold values from -6 to 6
- window_block: float32 [1024, 1024], P(('row', 'col')), may hold values from -1 to 2, as said below
Outputs:
- window_vectors: float32 [1024, 4096], P('row', 'col')
Inputs may be any that keep to these rules, and one draw needn't show every extreme that they name: window_block is zero above the diagonal; its diagonal lies in 1 to 2; entries below the diagonal are under 1 / sqrt(1024) in magnitude.
All inputs are finite; a program needn't handle non-finite values.
Results may differ from a plain program's by a relative error of at most 0.000082.
Values sent between devices are 32-bit elements; how exact they have to be, the bound alone decides.
A program may use at most 128 MiB of HBM per device.

v0:
```python
import jax
import jax.numpy as jnp
from jax import lax
from jax.sharding import PartitionSpec as P


def over_pieces(value, axis):
    blocks = lax.all_gather(value, axis)
    return blocks.sum(axis=0)


def per_device(tail_vectors, lower_panel, window_rhs, window_block):
    window = lower_panel.shape[1]
    block_full = lax.all_gather(window_block, ("row", "col"), axis=0, tiled=True)
    correction = lax.dot_general(
        lax.all_gather(lower_panel, "col", axis=0, tiled=True),
        tail_vectors,
        (((0,), (0,)), ((), ())),
        precision=lax.Precision.HIGHEST,
        preferred_element_type=jnp.float32,
    )
    row_share = window // lax.axis_size("row")
    offset = lax.axis_index("row") * row_share
    summand = -correction
    own_rows = lax.dynamic_slice_in_dim(summand, offset, row_share, 0) + window_rhs
    summand = lax.dynamic_update_slice_in_dim(summand, own_rows, offset, 0)
    right_side = over_pieces(summand, "row")
    solved = jax.scipy.linalg.solve_triangular(block_full, right_side, trans=1, lower=True)
    return lax.dynamic_slice_in_dim(solved, offset, row_share, 0)


def solution(mesh):
    in_specs = (P("row", "col"), P(("row", "col"), None), P("row", "col"), P(("row", "col"), None))
    out_specs = P("row", "col")
    return jax.shard_map(
        per_device, mesh=mesh, in_specs=in_specs, out_specs=out_specs, check_vma=False
    )
```

profile of v0, /device:TPU:1, one launch (start us, length us, event | category | flops | bytes accessed | tf_op | source)
XLA Modules:
  0.0 408.5 jit_solution(475037281372154553)
XLA Ops:
  6.5 0.7 all-gather.6.cloned.1.call-update
  7.3 0.7 all-gather.4.cloned.1.call-update
  8.1 198.9 %all-gather.6.cloned.1.call-done = f32[8064,1024]{1,0:T(8,128)} async-done(((f32[504,1024]{1,0:T(8,128)}), f32[8064,1024]{1,0:T(8,128)}) %all-gather.6.cloned.1.call-update) | async-done | bytes 33030160 | tf_op jit(solution)/shard_map/all_gather | solution.py:16
  207.0 57.1 %convolution_negate_fusion = f32[1024,256]{1,0:T(8,128)S(1)} fusion(f32[8064,1024]{1,0:T(8,128)} %all-gather.6.cloned.1.call-done, f32[8064,256]{1,0:T(8,128)} %param.4), kind=kOutput, calls=%fused_computation.4 | convolution fusion | flops 25367412736 | bytes 42336256 | tf_op jit(solution)/shard_map/dot_general | solution.py:15
  264.3 1.0 copy-done
  265.3 11.5 %all-gather.4.cloned.1.call-done = f32[1024,1024]{1,0:T(8,128)} async-done(((f32[8,1024]{1,0:T(8,128)}), f32[1024,1024]{1,0:T(8,128)}) %all-gather.4.cloned.1.call-update) | async-done | bytes 4194320 | tf_op jit(solution)/shard_map/all_gather | solution.py:14
  276.8 4.7 %fusion = f32[1024,1024]{1,0:T(8,128)} fusion(f32[1024,1024]{1,0:T(8,128)} %all-gather.4.cloned.1.call-done), kind=kLoop, calls=%fused_computation.3 | loop fusion | flops 2097152 | bytes 8388608 | tf_op jit(solution)/shard_map/jit(_solve_triangular)/triangular_solve | solution.py:28
  281.6 23.5 %while.1 = (s32[]{:T(128)}, f32[1024,1024]{1,0:T(8,128)}, s32[8,2]{0,1:T(2,128)S(1)}, f32[8,128,128]{2,1,0:T(8,128)S(1)}, s32[]{:T(128)}) while((s32[]{:T(128)}, f32[1024,1024]{1,0:T(8,128)}, s32[8,2]{0,1:T(2,128)S(1)}, f32[8,128,128]{2,1,0:T(8,128)S(1)}, s32[]{:T(128)}) %tuple.22), condition=%wide.while_cond, body=%wide.while_body.sunk | while | flops 2 | bytes 131189 | solution.py:28
  281.6 0.1 constant_dynamic-slice_fusion.3
  281.6 0.6 fusion.49
  282.2 2.3 bitcast_dynamic-update-slice_fusion.3
  284.5 0.1 constant_dynamic-slice_fusion.3
  284.6 0.6 fusion.49
  285.2 2.3 bitcast_dynamic-update-slice_fusion.3
  287.5 0.1 constant_dynamic-slice_fusion.3
  287.6 0.6 fusion.49
  288.2 2.3 bitcast_dynamic-update-slice_fusion.3
  290.4 0.1 constant_dynamic-slice_fusion.3
  290.5 0.6 fusion.49
  291.1 2.3 bitcast_dynamic-update-slice_fusion.3
  293.4 0.1 constant_dynamic-slice_fusion.3
  293.4 0.6 fusion.49
  294.0 2.3 bitcast_dynamic-update-slice_fusion.3
  296.3 0.1 constant_dynamic-slice_fusion.3
  296.4 0.6 fusion.49
  297.0 2.3 bitcast_dynamic-update-slice_fusion.3
  299.3 0.6 fusion.49
  299.9 2.3 bitcast_dynamic-update-slice_fusion.3
  302.3 0.6 fusion.49
  302.8 2.2 bitcast_dynamic-update-slice_fusion.3
  305.0 78.6 %custom-call.4 = f32[8,128,128]{1,2,0:T(8,128)S(1)} custom-call(f32[8,128,128]{2,1,0:T(8,128)S(1)} %get-tuple-element.12), custom_call_target="InvertDiagBlocksLowerTriangular" | custom-call | tf_op jit(solution)/shard_map/jit(_solve_triangular)/triangular_solve | solution.py:28
  383.7 4.1 reduce_sum.9
  387.7 0.3 fusion.21
  388.0 1.1 convolution_subtract_fusion.5
  389.2 0.3 fusion.25
  389.4 1.3 convolution_subtract_fusion.3
  390.7 0.3 fusion.26
  391.0 1.4 convolution_subtract_fusion.2
  392.4 0.3 fusion.27
  392.7 1.6 convolution_subtract_fusion.1
  394.3 0.3 constant_dynamic-update-slice_fusion.4
  394.6 1.7 convolution_subtract_fusion
  396.3 0.3 constant_dynamic-update-slice_fusion.10
  396.7 1.8 convolution_subtract_fusion.4
  398.5 0.3 constant_dynamic-update-slice_fusion.17
  398.9 2.0 convolution_subtract_fusion.6
  400.9 0.3 convolution_dynamic-update-slice_fusion
  401.3 0.7 constant_dynamic-slice_fusion.1
  (37 shorter events, 0.6 us)
Async XLA Ops:
  6.5 200.4 %all-gather.6.cloned.1.call-start = ((), (), s32[]{:S(2)}) async-start(), calls=%async_computation.1 | async-start | bytes 35094528 | tf_op jit(solution)/shard_map/all_gather | solution.py:16
  7.3 269.6 %all-gather.4.cloned.1.call-start = ((), (), s32[]{:S(2)}) async-start(), calls=%async_computation | async-start | bytes 4227072 | tf_op jit(solution)/shard_map/all_gather | solution.py:14
  8.0 375.7 %all-gather.8.cloned.1.call-start = ((), (), s32[]{:S(2)}) async-start(), calls=%async_computation.2 | async-start | bytes 9437184 | tf_op jit(solution)/shard_map/all_gather | solution.py:8
  8.1 256.1 %copy-start.1 = (f32[128,256]{1,0:T(8,128)S(1)}, f32[128,256]{1,0:T(8,128)}, u32[]{:S(2)}) copy-start(f32[128,256]{1,0:T(8,128)} %param.6) | copy-start | bytes 393220
  264.2 1.1 copy-start
Sparse Core Ops, SparseCore 0:
  9.5 197.4 all-gather.5
  210.1 66.6 all-gather.3
  278.6 47.4 all-gather.7
where the time goes:
time: 409 us
  waiting for transfers between devices  212 us (52%)
  other arithmetic  87.4 us (21%)
  matrix products  70.2 us (17%)
  local copies, waits for them, and re-layouts  25.4 us (6%)
  between operations  13.5 us (3%)
    all_gather x1, waiting for transfers between devices, per_device(): lax.all_gather(lower_panel, 'col', axis=0, tiled=True)  199 us
    another operation x3, other arithmetic, per_device(): jax.scipy.linalg.solve_triangular(block_full, right_side, trans=1, lower=...  83.3 us
    dot_general x1, matrix products, per_device(): lax.dot_general(lax.all_gather(lower_panel, 'col', axis=0, tiled=True), t...  57.1 us
    another operation x24, local copies, waits for them, and re-layouts  23.3 us
    another operation x15, matrix products, per_device(): jax.scipy.linalg.solve_triangular(block_full, right_side, trans=1, lower=...  13 us
    all_gather x1, waiting for transfers between devices, per_device(): lax.all_gather(window_block, ('row', 'col'), axis=0, tiled=True)  11.5 us
  transfers between devices with their start and end apart: 3, of which 2 were waited for; matrix products, arithmetic and copies ran while one was open for 40% of the time, Pallas kernels for 0%

commit v1 on v0

v1 whole, which is shorter than its diff:
```python
import functools

import jax
import jax.numpy as jnp
from jax import lax
from jax.experimental import pallas as pl
from jax.experimental.pallas import tpu as pltpu
from jax.sharding import PartitionSpec as P

F32, BF16 = jnp.float32, jnp.bfloat16
HIGHEST = lax.Precision.HIGHEST
SEG = 504
PAD = 512
WIN = 1024
COLS = 256
BLK = 128


def split(value):
    high = value.astype(BF16)
    return high, (value - high.astype(F32)).astype(BF16)


def dot(a, b, precision=None):
    return jnp.dot(a, b, preferred_element_type=F32, precision=precision)


def kernel(
    tail, panel, rhs, block, out,
    tbuf, fwd, lbuf, lsplit, tt, acc, wrow, gfull, gsplit, rhs_in,
    r1, part, ring1, ring2, psum, r3, xs, obuf,
    send_sem, recv_sem, local_sem,
):
    row, col = lax.axis_index("row"), lax.axis_index("col")
    x, core = row // 2, row % 2
    z, y = col // 4, col % 4
    counter = [0]
    started = []

    def where(dx=0, dc=0, dz=0, dy=0):
        new_row = 2 * ((x + dx + 4) % 4) + (core + dc) % 2
        new_col = 4 * ((z + dz + 4) % 4) + (y + dy + 4) % 4
        return (new_row, new_col)

    def copy(src, dst, target):
        index = counter[0]
        counter[0] += 1
        made = pltpu.make_async_remote_copy(
            src_ref=src,
            dst_ref=dst,
            send_sem=send_sem.at[index],
            recv_sem=recv_sem.at[index],
            device_id=target,
            device_id_type=pl.DeviceIdType.MESH,
        )
        made.start()
        started.append(made)
        return made

    def tail_rows(e, dy):
        start = (4 * ((z - e + 4) % 4) + (y + dy + 4) % 4) * SEG
        return tail.at[pl.ds(pl.multiple_of(start, 8), SEG), :]

    partners = [where(dy=i) for i in (1, 2, 3)] + [where(dz=i) for i in (1, 2, 3)]
    partners += [where(dx=i, dc=j) for i in range(4) for j in range(2) if (i, j) != (0, 0)]
    barrier = pltpu.get_barrier_semaphore()
    for partner in partners:
        pl.semaphore_signal(barrier, inc=1, device_id=partner, device_id_type=pl.DeviceIdType.MESH)
    pl.semaphore_wait(barrier, len(partners))

    mine = pl.ds(pl.multiple_of(col * 8, 8), 8)
    over_y = [copy(block, wrow.at[mine, :], where(dy=i)) for i in (1, 3, 2)]

    far_up = [copy(tail_rows(e, 2), fwd.at[i], where(dy=1)) for i, e in enumerate((0, 1))]
    far_down = [copy(tail_rows(e, 2), fwd.at[2 + i], where(dy=3)) for i, e in enumerate((3, 2))]
    near_up, near_down = {}, {}
    for e in (0, 1, 3, 2):
        near_up[e] = copy(tail_rows(e, 1), tbuf.at[1, e, pl.ds(0, SEG), :], where(dy=1))
        near_down[e] = copy(tail_rows(e, 3), tbuf.at[3, e, pl.ds(0, SEG), :], where(dy=3))

    local = []

    def bring(src, dst):
        made = pltpu.make_async_copy(src, dst, local_sem.at[len(local)])
        made.start()
        local.append(made)
        return made

    own_block = bring(block, wrow.at[mine, :])
    own_panel = bring(panel, lbuf.at[0, pl.ds(0, SEG), :])
    own_rhs = bring(rhs, rhs_in)
    own_tail = {e: bring(tail_rows(e, 0), tbuf.at[0, e, pl.ds(0, SEG), :]) for e in range(4)}

    for e in range(4):
        lbuf[e, SEG:, :] = jnp.zeros((PAD - SEG, WIN), F32)
        for d in range(4):
            tbuf[d, e, SEG:, :] = jnp.zeros((PAD - SEG, COLS), F32)

    own_block.wait()
    for made in over_y:
        made.wait_recv()
    quarter = pl.ds(pl.multiple_of(z * 32, 32), 32)
    over_z = [copy(wrow.at[quarter, :], wrow.at[quarter, :], where(dz=i)) for i in (1, 3, 2)]

    top, bottom = pl.ds(0, 256), pl.ds(256, SEG - 256)
    up_first = copy(panel.at[top, :], lbuf.at[1, top, :], where(dz=1))
    down_first = copy(panel.at[bottom, :], lbuf.at[3, bottom, :], where(dz=3))
    up_second = copy(panel.at[bottom, :], lbuf.at[1, bottom, :], where(dz=1))
    down_second = copy(panel.at[top, :], lbuf.at[3, top, :], where(dz=3))

    for made in over_z:
        made.wait_recv()

    rows = lax.broadcasted_iota(jnp.int32, (BLK, BLK), 0)
    cols = lax.broadcasted_iota(jnp.int32, (BLK, BLK), 1)
    eye = jnp.where(rows == cols, 1.0, 0.0).astype(F32)
    own_cols = pl.ds(pl.multiple_of(row * BLK, BLK), BLK)
    diagonal = wrow[:, own_cols]
    on_diag = jnp.where(rows == cols, diagonal, 0.0)
    diag_rows = jnp.sum(on_diag, axis=1, keepdims=True)
    diag_cols = jnp.sum(on_diag, axis=0, keepdims=True)
    lower = jnp.where(rows > cols, diagonal, 0.0) / diag_rows

    inverse, power = eye - lower, dot(lower, lower, HIGHEST)
    for _ in range(6):
        both = dot(jnp.concatenate([inverse, power], axis=0), power, HIGHEST)
        inverse, power = inverse + both[:BLK], both[BLK:]
    inverse = inverse / diag_cols
    gfull[row] = dot(inverse, wrow[...], HIGHEST)
    gfull[row, :, own_cols] = inverse
    over_x = [copy(gfull.at[row], gfull.at[row], where(dx=i)) for i in (1, 3, 2)]
    across = [copy(gfull.at[row], gfull.at[row], where(dc=1))]

    def split_panel(e):
        @pl.loop(0, 4)
        def _(step):
            at = pl.ds(pl.multiple_of(step * BLK, BLK), BLK)
            high, low = split(lbuf[e, at, :])
            lsplit[e, pl.ds(pl.multiple_of(step * BLK, BLK), BLK), :] = low
            lsplit[e, pl.ds(pl.multiple_of(PAD + step * BLK, BLK), BLK), :] = high

    def product(d, e, first):
        @pl.loop(0, 4)
        def _(step):
            base = pl.multiple_of(step * BLK, BLK)
            high, low = split(tbuf[d, e, pl.ds(base, BLK), :].T)
            tt[:, pl.ds(base, BLK)] = high
            tt[:, pl.ds(pl.multiple_of(PAD + step * BLK, BLK), BLK)] = low

        @pl.loop(0, 4)
        def _(step):
            at = pl.ds(pl.multiple_of(step * 256, 256), 256)
            value = dot(tt[...], lsplit[e, :, at]) + dot(tt[:, :PAD], lsplit[e, PAD:, at])
            if first:
                acc[d, :, at] = value
            else:
                acc[d, :, at] += value

    own_panel.wait()
    split_panel(0)
    own_tail[0].wait()
    product(0, 0, True)
    own_rhs.wait()
    acc[0, :, own_cols] += -rhs_in[...].T

    far = {}
    for i, e in enumerate((0, 1)):
        far_up[i].wait_recv()
        far[e] = copy(fwd.at[i], tbuf.at[2, e, pl.ds(0, SEG), :], where(dy=1))
    for i, e in enumerate((3, 2)):
        far_down[i].wait_recv()
        far[e] = copy(fwd.at[2 + i], tbuf.at[2, e, pl.ds(0, SEG), :], where(dy=3))
    up_first.wait_recv()
    up_on = copy(lbuf.at[1, top, :], lbuf.at[2, top, :], where(dz=1))
    down_first.wait_recv()
    down_on = copy(lbuf.at[3, bottom, :], lbuf.at[2, bottom, :], where(dz=3))

    for made, i in zip(over_x, (1, 3, 2)):
        made.wait_recv()
        slot = 2 * ((x - i + 4) % 4) + core
        across.append(copy(gfull.at[slot], gfull.at[slot], where(dc=1)))

    near_up[0].wait_recv()
    product(1, 0, True)
    near_down[0].wait_recv()
    product(3, 0, True)

    for made in across:
        made.wait_recv()

    @pl.loop(0, 8)
    def _(step):
        high, low = split(gfull[step])
        gsplit[0, step] = high
        gsplit[1, step] = low

    for e in (1, 3):
        own_tail[e].wait()
    up_second.wait_recv()
    split_panel(1)
    product(0, 1, False)
    down_second.wait_recv()
    split_panel(3)
    product(0, 3, False)
    for e in (1, 3):
        near_up[e].wait_recv()
        product(1, e, False)
        near_down[e].wait_recv()
        product(3, e, False)

    up_on.wait_recv()
    down_on.wait_recv()
    split_panel(2)

    pair, first_hop, second_hop, third = {}, {}, {}, {}
    keep = pl.ds(pl.multiple_of(core * BLK, BLK), BLK)
    give = pl.ds(pl.multiple_of((1 - core) * BLK, BLK), BLK)
    upper, under = pl.ds(0, 16), pl.ds(16, 16)
    x_up, x_down, x_far = (x + 1) % 4, (x + 3) % 4, (x + 2) % 4

    def to_pair(d):
        pair[d] = copy(acc.at[d, give, :], r1.at[d], where(dc=1))

    def to_ring(d):
        pair[d].wait_recv()
        part[d] = (acc[d, keep, :] + r1[d]).reshape(4, 32, WIN)
        first_hop[d] = (
            copy(part.at[d, x_far, upper, :], ring1.at[d, 0], where(dx=1)),
            copy(part.at[d, x_far, under, :], ring1.at[d, 1], where(dx=3)),
        )

    def round_ring(d):
        first_hop[d][0].wait_recv()
        part[d, x_up, upper, :] += ring1[d, 0]
        up = copy(part.at[d, x_up], ring2.at[d, 0], where(dx=1))
        first_hop[d][1].wait_recv()
        part[d, x_down, under, :] += ring1[d, 1]
        second_hop[d] = (up, copy(part.at[d, x_down], ring2.at[d, 1], where(dx=3)))

    def from_ring(d):
        second_hop[d][0].wait_recv()
        second_hop[d][1].wait_recv()
        psum[d] = part[d, x] + ring2[d, 0] + ring2[d, 1]
        if d:
            third[d] = copy(psum.at[d], r3.at[d], where(dy=-d))

    own_tail[2].wait()
    product(0, 2, False)
    to_pair(0)
    near_up[2].wait_recv()
    product(1, 2, False)
    to_pair(1)
    to_ring(0)
    near_down[2].wait_recv()
    product(3, 2, False)
    to_pair(3)
    to_ring(1)
    to_ring(3)
    far[0].wait_recv()
    product(2, 0, True)
    for d in (0, 1, 3):
        round_ring(d)
    far[3].wait_recv()
    product(2, 3, False)
    for d in (0, 1, 3):
        from_ring(d)
    for e in (1, 2):
        far[e].wait_recv()
        product(2, e, False)
    to_pair(2)
    to_ring(2)
    round_ring(2)
    from_ring(2)

    total = psum[0]
    for d in (1, 3, 2):
        third[d].wait_recv()
        total += r3[d]

    left = -total
    for j in range(7, -1, -1):
        high, low = split(left[:, j * BLK : (j + 1) * BLK])
        width = (j + 1) * BLK
        both = dot(jnp.concatenate([high, low], axis=0), gsplit[0, j, :, :width])
        step = both[:32] + both[32:] + dot(high, gsplit[1, j, :, :width])
        xs[j] = step[:, j * BLK :]
        if j:
            left = left[:, : j * BLK] - step[:, : j * BLK]

    own = pl.ds(pl.multiple_of(core * BLK + x * 32, 32), 32)
    obuf[own, :] = xs[row]
    spread = []
    for i in range(4):
        for j in range(2):
            if (i, j) != (0, 0):
                target = where(dx=i, dc=j)
                spread.append(copy(xs.at[target[0]], obuf.at[own, :], target))
    for made in spread:
        made.wait_recv()
    out[...] = obuf[...].T
    for made in started:
        made.wait_send()


COPIES = 80


def per_device(tail_vectors, lower_panel, window_rhs, window_block):
    anywhere = pl.BlockSpec(memory_space=pl.ANY)
    return pl.pallas_call(
        kernel,
        name="window_solve",
        out_shape=jax.ShapeDtypeStruct((BLK, COLS), F32),
        in_specs=[anywhere] * 4,
        out_specs=pl.BlockSpec(memory_space=pltpu.VMEM),
        scratch_shapes=[
            pltpu.VMEM((4, 4, PAD, COLS), F32),
            pltpu.VMEM((4, SEG, COLS), F32),
            pltpu.VMEM((4, PAD, WIN), F32),
            pltpu.VMEM((4, 2 * PAD, WIN), BF16),
            pltpu.VMEM((COLS, 2 * PAD), BF16),
            pltpu.VMEM((4, COLS, WIN), F32),
            pltpu.VMEM((BLK, WIN), F32),
            pltpu.VMEM((8, BLK, WIN), F32),
            pltpu.VMEM((2, 8, BLK, WIN), BF16),
            pltpu.VMEM((BLK, COLS), F32),
            pltpu.VMEM((4, BLK, WIN), F32),
            pltpu.VMEM((4, 4, 32, WIN), F32),
            pltpu.VMEM((4, 2, 16, WIN), F32),
            pltpu.VMEM((4, 2, 32, WIN), F32),
            pltpu.VMEM((4, 32, WIN), F32),
            pltpu.VMEM((4, 32, WIN), F32),
            pltpu.VMEM((8, 32, BLK), F32),
            pltpu.VMEM((COLS, BLK), F32),
            pltpu.SemaphoreType.DMA((COPIES,)),
            pltpu.SemaphoreType.DMA((COPIES,)),
            pltpu.SemaphoreType.DMA((8,)),
        ],
        compiler_params=pltpu.CompilerParams(
            collective_id=0, has_side_effects=True, vmem_limit_bytes=62 * 1024 * 1024
        ),
    )(tail_vectors, lower_panel, window_rhs, window_block)


def solution(mesh):
    in_specs = (P("row", "col"), P(("row", "col"), None), P("row", "col"), P(("row", "col"), None))
    return jax.shard_map(
        per_device, mesh=mesh, in_specs=in_specs, out_specs=P("row", "col"), check_vma=False
    )
```

time: 409 us -> 136 us (0.33)
  waiting for transfers between devices: 212 us -> 0 us
  Pallas kernels: 0 us -> 134 us
  other arithmetic: 87.4 us -> 0 us
  matrix products: 70.2 us -> 0 us
  local copies, waits for them, and re-layouts: 25.4 us -> 1.57 us
  between operations: 13.5 us -> 0.01 us
    all_gather x3 -> x0, waiting for transfers between devices: 210 us -> none  [the longest x1 199 us: per_device(): lax.all_gather(lower_panel, 'col', axis=0, tiled=True)]
    pallas_call x0 -> x1, Pallas kernels: none -> 134 us  [per_device(): pl.pallas_call(kernel, name='window_solve', out_shape=jax.ShapeDtypeStruc...]
    another operation x3 -> x0, other arithmetic: 83.3 us -> none  [per_device(): jax.scipy.linalg.solve_triangular(block_full, right_side, trans=1, lower=...]
    dot_general x1 -> x0, matrix products: 57.1 us -> none  [per_device(): lax.dot_general(lax.all_gather(lower_panel, 'col', axis=0, tiled=True), t...]
    another operation x29 -> x0, local copies, waits for them, and re-layouts: 23.4 us -> none
    another operation x15 -> x0, matrix products: 13 us -> none  [per_device(): jax.scipy.linalg.solve_triangular(block_full, right_side, trans=1, lower=...]
  transfers between devices with their start and end apart: 3 -> 0, of which waited for: 2 -> 0; matrix products, arithmetic and copies ran while one was open for 40% -> 0% of each run, Pallas kernels for 0% -> 0%
where the time goes in v1:
time: 136 us
  Pallas kernels  134 us (99%)
  local copies, waits for them, and re-layouts  1.57 us (1%)
    pallas_call x1, Pallas kernels, per_device(): pl.pallas_call(kernel, name='window_solve', out_shape=jax.ShapeDtypeStruc...  134 us

profile of v1, /device:TPU:1, one launch (start us, length us, event | category | flops | bytes accessed | tf_op | source)
XLA Modules:
  0.0 135.5 jit_solution(6192041520465355375)
XLA Ops:
  0.0 134.0 %window_solve.1 = f32[128,256]{1,0:T(8,128)} custom-call(f32[8064,256]{1,0:T(8,128)} %tail.1, f32[504,1024]{1,0:T(8,128)} %panel.1, f32[128,256]{1,0:T(8,128)} %rhs.1, f32[8,1024]{1,0:T(8,128)} %block.1), custom_call_target="tpu_custom_call" | custom-call | tf_op jit(solution)/shard_map/window_solve/pallas_call | solution.py:310
  134.0 1.6 %copy.6 = f32[128,256]{1,0:T(8,128)} copy(f32[128,256]{1,0:T(8,128)} %window_solve.1) | data formatting | bytes 262144

commit v2 on v0

v2 whole, which is shorter than its diff:
```python
import jax
import jax.numpy as jnp
from jax import lax
from jax.experimental import pallas as pl
from jax.experimental.pallas import tpu as pltpu
from jax.sharding import PartitionSpec as P

F32, BF16 = jnp.float32, jnp.bfloat16
HIGHEST = lax.Precision.HIGHEST
SEG = 504
LEN = (256, 248)
PART = 256
DEEP = 4 * PART
WIN = 1024
COLS = 256
BLK = 128
QUARTER = 16
CHUNKS = [(None, 0, 0), (None, 0, 1)] + [(p, d, h) for h in range(2) for d in (1, 3, 2) for p in range(2)]
NUMBER = {chunk: q for q, chunk in enumerate(CHUNKS)}
COPIES = 112


def split(value):
    high = value.astype(BF16)
    return high, (value - high.astype(F32)).astype(BF16)


def dot(a, b, precision=None):
    return jnp.dot(a, b, preferred_element_type=F32, precision=precision)


def aligned(start, size, unit):
    return pl.ds(pl.multiple_of(start, unit), size)


def kernel(
    tail, panel, rhs, block, out,
    tbuf, lbuf, lsplit, tt, cbuf, wrow, gfull, gsplit, rhs_in,
    r1, part, ring, psum, r3, xs, obuf,
    send_sem, recv_sem, local_sem,
):
    row, col = lax.axis_index("row"), lax.axis_index("col")
    x, core = row // 2, row % 2
    z, y = col // 4, col % 4
    counter = [0]
    started = []

    def where(dx=0, dc=0, dz=0, dy=0):
        new_row = 2 * ((x + dx + 4) % 4) + (core + dc) % 2
        new_col = 4 * ((z + dz + 4) % 4) + (y + dy + 4) % 4
        return (new_row, new_col)

    def along(p, step):
        return where(dy=step) if p == 0 else where(dz=step)

    def across(p, step):
        return along(1 - p, step)

    place = (z, y)

    def copy(src, dst, target):
        index = counter[0]
        counter[0] += 1
        made = pltpu.make_async_remote_copy(
            src_ref=src,
            dst_ref=dst,
            send_sem=send_sem.at[index],
            recv_sem=recv_sem.at[index],
            device_id=target,
            device_id_type=pl.DeviceIdType.MESH,
        )
        made.start()
        started.append(made)
        return made

    local = []

    def bring(src, dst):
        made = pltpu.make_async_copy(src, dst, local_sem.at[len(local)])
        made.start()
        local.append(made)
        return made

    def piece(p, step, h):
        columns = pl.ds(h * BLK, BLK)
        if p == 0:
            return tail.at[:, (y + step) % 4, pl.ds(0, LEN[0]), columns]
        return tail.at[(z + step) % 4, :, pl.ds(LEN[0], LEN[1]), columns]

    def landing(p, d, h):
        return tbuf.at[p, d, h, :, pl.ds(0, LEN[p]), :]

    partners = [where(dy=i) for i in (1, 2, 3)] + [where(dz=i) for i in (1, 2, 3)]
    partners += [where(dx=i, dc=j) for i in range(4) for j in range(2) if (i, j) != (0, 0)]
    barrier = pltpu.get_barrier_semaphore()
    for partner in partners:
        pl.semaphore_signal(barrier, inc=1, device_id=partner, device_id_type=pl.DeviceIdType.MESH)
    pl.semaphore_wait(barrier, len(partners))

    mine = aligned(col * 8, 8, 8)
    over_y = [copy(block, wrow.at[mine, :], where(dy=i)) for i in (1, 3, 2)]

    def half(p, side):
        return pl.ds(0, 128) if side == 0 else pl.ds(128, LEN[p] - 128)

    def send_panel(p, step, side):
        src = pl.ds(p * PART + half(p, side).start, half(p, side).size)
        return copy(panel.at[src, :], lbuf.at[p, place[p], half(p, side), :], across(p, step))

    first = [(send_panel(p, 1, 0), send_panel(p, 3, 1)) for p in (1, 0)]
    own_block = bring(block, wrow.at[mine, :])
    own_panel = [
        bring(panel.at[pl.ds(p * PART, LEN[p]), :], lbuf.at[p, place[p], pl.ds(0, LEN[p]), :]) for p in range(2)
    ]
    own_rhs = bring(rhs, rhs_in)
    own_tail = [bring(piece(p, 0, h), landing(p, 0, h)) for p in range(2) for h in range(2)]
    second = [(send_panel(1, 1, 1), send_panel(1, 3, 0))]

    for i in range(4):
        lbuf[1, i, LEN[1] :, :] = jnp.zeros((PART - LEN[1], WIN), F32)
        for d in range(4):
            for h in range(2):
                tbuf[1, d, h, i, LEN[1] :, :] = jnp.zeros((PART - LEN[1], BLK), F32)

    own_block.wait()
    for made in over_y:
        made.wait_recv()
    quarter = aligned(z * 32, 32, 32)
    over_z = [copy(wrow.at[quarter, :], wrow.at[quarter, :], where(dz=i)) for i in (1, 3, 2)]
    second.append((send_panel(0, 1, 1), send_panel(0, 3, 0)))

    onward = []
    for p, (up, down) in zip((1, 0), first):
        below, above = (place[p] + 3) % 4, (place[p] + 1) % 4
        up.wait_recv()
        at = lbuf.at[p, below, half(p, 0), :]
        onward.append(copy(at, at, across(p, 1)))
        down.wait_recv()
        at = lbuf.at[p, above, half(p, 1), :]
        onward.append(copy(at, at, across(p, 3)))

    pieces = {}
    for h in range(2):
        for d in (1, 3, 2):
            for p in range(2):
                pieces[p, d, h] = copy(piece(p, d, h), landing(p, d, h), along(p, d))

    for made in over_z:
        made.wait_recv()

    rows = lax.broadcasted_iota(jnp.int32, (BLK, BLK), 0)
    cols = lax.broadcasted_iota(jnp.int32, (BLK, BLK), 1)
    eye = jnp.where(rows == cols, 1.0, 0.0).astype(F32)
    own_cols = aligned(row * BLK, BLK, BLK)
    diagonal = wrow[:, own_cols]
    on_diag = jnp.where(rows == cols, diagonal, 0.0)
    diag_rows = jnp.sum(on_diag, axis=1, keepdims=True)
    diag_cols = jnp.sum(on_diag, axis=0, keepdims=True)
    lower = jnp.where(rows > cols, diagonal, 0.0) / diag_rows
    inverse, power = eye - lower, dot(lower, lower, HIGHEST)
    for _ in range(6):
        both = dot(jnp.concatenate([inverse, power], axis=0), power, HIGHEST)
        inverse, power = inverse + both[:BLK], both[BLK:]
    inverse = inverse / diag_cols
    gfull[row] = dot(inverse, wrow[...], HIGHEST)
    gfull[row, :, own_cols] = inverse
    over_x = [copy(gfull.at[row], gfull.at[row], where(dx=i)) for i in (1, 3, 2)]
    to_other = [copy(gfull.at[row], gfull.at[row], where(dc=1))]

    for made in own_panel:
        made.wait()
    for up, down in second:
        up.wait_recv()
        down.wait_recv()
    for made in onward:
        made.wait_recv()

    @pl.loop(0, 2)
    def _(p):
        @pl.loop(0, 8)
        def _(step):
            high, low = split(lbuf[p, step // 2, aligned((step % 2) * BLK, BLK, BLK), :])
            lsplit[p, aligned(step * BLK, BLK, BLK), :] = low
            lsplit[p, aligned(DEEP + step * BLK, BLK, BLK), :] = high

    def product(p, sources, store):
        for i, (d, h) in enumerate(sources):

            @pl.loop(0, 4)
            def _(step):
                high, low = split(tbuf[p, d, h, step].T)
                tt[pl.ds(i * BLK, BLK), aligned(step * PART, PART, PART)] = high
                tt[pl.ds(i * BLK, BLK), aligned(DEEP + step * PART, PART, PART)] = low

        height = pl.ds(0, len(sources) * BLK)

        @pl.loop(0, 4)
        def _(step):
            at = aligned(step * 256, 256, 256)
            value = dot(tt[height, :], lsplit[p, :, at]) + dot(tt[height, :DEEP], lsplit[p, DEEP:, at])
            for i in range(len(sources)):
                store(i, at, value[i * BLK : (i + 1) * BLK])

    keep, give = aligned(core * 64, 64, 64), aligned((1 - core) * 64, 64, 64)
    pair, ringed, third = {}, {}, {}

    def to_pair(q):
        pair[q] = copy(cbuf.at[q, give, :], r1.at[q], where(dc=1))

    def to_ring(q):
        pair[q].wait_recv()
        part[q] = (cbuf[q, keep, :] + r1[q]).reshape(4, QUARTER, WIN)
        ringed[q] = [copy(part.at[q, (x + i) % 4], ring.at[q, i - 1], where(dx=i)) for i in (2, 1, 3)]

    def from_ring(q):
        for made in ringed[q]:
            made.wait_recv()
        psum[q] = part[q, x] + ring[q, 0] + ring[q, 1] + ring[q, 2]
        p, d, _ = CHUNKS[q]
        if d:
            third[q] = copy(psum.at[q], r3.at[q - 2], along(p, -d))

    def chunk_product(p, sources):
        numbers = [NUMBER[p, d, h] for d, h in sources]
        for d, h in sources:
            pieces[p, d, h].wait_recv()

        def store(i, at, value):
            cbuf[numbers[i], :, at] = value

        product(p, sources, store)
        for q in numbers:
            to_pair(q)
        return numbers

    def store_own(i, at, value):
        cbuf[i, :, at] = value

    def add_own(i, at, value):
        cbuf[i, :, at] += value

    for made in own_tail:
        made.wait()
    product(0, [(0, 0), (0, 1)], store_own)
    product(1, [(0, 0), (0, 1)], add_own)
    own_rhs.wait()
    turned = rhs_in[...].T
    for h in range(2):
        cbuf[h, :, own_cols] += -turned[h * BLK : (h + 1) * BLK]
        to_pair(h)
    for made, i in zip(over_x, (1, 3, 2)):
        made.wait_recv()
        slot = 2 * ((x - i + 4) % 4) + core
        to_other.append(copy(gfull.at[slot], gfull.at[slot], where(dc=1)))
    to_ring(0)
    to_ring(1)

    a = chunk_product(0, [(1, 0), (3, 0)])
    b = chunk_product(1, [(1, 0), (3, 0)])
    for q in a + b:
        to_ring(q)

    for made in to_other:
        made.wait_recv()

    @pl.loop(0, 8)
    def _(step):
        high, low = split(gfull[step])
        gsplit[0, step] = high
        gsplit[1, step] = low

    from_ring(0)
    from_ring(1)
    c = chunk_product(0, [(2, 0)]) + chunk_product(1, [(2, 0)])
    for q in a + b:
        from_ring(q)
    for q in c:
        to_ring(q)
    a = chunk_product(0, [(1, 1), (3, 1)])
    b = chunk_product(1, [(1, 1), (3, 1)])
    for q in c:
        from_ring(q)
    for q in a + b:
        to_ring(q)
    c = chunk_product(0, [(2, 1)])
    for q in a + b:
        from_ring(q)
    c += chunk_product(1, [(2, 1)])
    for q in c:
        to_ring(q)
    totals = []
    for h in range(2):
        if h:
            for q in c:
                from_ring(q)
        total = psum[h]
        for d in (1, 3, 2):
            for p in range(2):
                q = NUMBER[p, d, h]
                third[q].wait_recv()
                total += r3[q - 2]
        totals.append(total)

    left = -jnp.concatenate(totals, axis=0)
    for j in range(7, -1, -1):
        high, low = split(left[:, j * BLK : (j + 1) * BLK])
        width = (j + 1) * BLK
        both = dot(jnp.concatenate([high, low], axis=0), gsplit[0, j, :, :width])
        step = both[:32] + both[32:] + dot(high, gsplit[1, j, :, :width])
        xs[j] = step[:, j * BLK :].reshape(2, QUARTER, BLK)
        if j:
            left = left[:, : j * BLK] - step[:, : j * BLK]

    own = aligned(core * 64 + x * QUARTER, QUARTER, QUARTER)
    obuf[:, own, :] = xs[row]
    spread = []
    for i in range(4):
        for j in range(2):
            if (i, j) != (0, 0):
                target = where(dx=i, dc=j)
                spread.append(copy(xs.at[target[0]], obuf.at[:, own, :], target))
    for made in spread:
        made.wait_recv()
    out[...] = obuf[...].reshape(COLS, BLK).T
    for made in started:
        made.wait_send()


def per_device(tail_vectors, lower_panel, window_rhs, window_block):
    anywhere = pl.BlockSpec(memory_space=pl.ANY)
    count = len(CHUNKS)
    return pl.pallas_call(
        kernel,
        name="window_solve",
        out_shape=jax.ShapeDtypeStruct((BLK, COLS), F32),
        in_specs=[anywhere] * 4,
        out_specs=pl.BlockSpec(memory_space=pltpu.VMEM),
        scratch_shapes=[
            pltpu.VMEM((2, 4, 2, 4, PART, BLK), F32),
            pltpu.VMEM((2, 4, PART, WIN), F32),
            pltpu.VMEM((2, 2 * DEEP, WIN), BF16),
            pltpu.VMEM((COLS, 2 * DEEP), BF16),
            pltpu.VMEM((count, BLK, WIN), F32),
            pltpu.VMEM((BLK, WIN), F32),
            pltpu.VMEM((8, BLK, WIN), F32),
            pltpu.VMEM((2, 8, BLK, WIN), BF16),
            pltpu.VMEM((BLK, COLS), F32),
            pltpu.VMEM((count, 64, WIN), F32),
            pltpu.VMEM((count, 4, QUARTER, WIN), F32),
            pltpu.VMEM((count, 3, QUARTER, WIN), F32),
            pltpu.VMEM((count, QUARTER, WIN), F32),
            pltpu.VMEM((count - 2, QUARTER, WIN), F32),
            pltpu.VMEM((8, 2, QUARTER, BLK), F32),
            pltpu.VMEM((2, BLK, BLK), F32),
            pltpu.SemaphoreType.DMA((COPIES,)),
            pltpu.SemaphoreType.DMA((COPIES,)),
            pltpu.SemaphoreType.DMA((8,)),
        ],
        compiler_params=pltpu.CompilerParams(
            collective_id=0, has_side_effects=True, vmem_limit_bytes=62 * 1024 * 1024
        ),
    )(tail_vectors.reshape(4, 4, SEG, COLS), lower_panel, window_rhs, window_block)


def solution(mesh):
    in_specs = (P("row", "col"), P(("row", "col"), None), P("row", "col"), P(("row", "col"), None))
    return jax.shard_map(
        per_device, mesh=mesh, in_specs=in_specs, out_specs=P("row", "col"), check_vma=False
    )
```

time: 409 us -> 128 us (0.31)
  waiting for transfers between devices: 212 us -> 0 us
  Pallas kernels: 0 us -> 126 us
  other arithmetic: 87.4 us -> 0 us
  matrix products: 70.2 us -> 0 us
  local copies, waits for them, and re-layouts: 25.4 us -> 1.57 us
  between operations: 13.5 us -> 0.01 us
    all_gather x3 -> x0, waiting for transfers between devices: 210 us -> none  [the longest x1 199 us: per_device(): lax.all_gather(lower_panel, 'col', axis=0, tiled=True)]
    pallas_call x0 -> x1, Pallas kernels: none -> 126 us  [per_device(): pl.pallas_call(kernel, name='window_solve', out_shape=jax.ShapeDtypeStruc...]
    another operation x3 -> x0, other arithmetic: 83.3 us -> none  [per_device(): jax.scipy.linalg.solve_triangular(block_full, right_side, trans=1, lower=...]
    dot_general x1 -> x0, matrix products: 57.1 us -> none  [per_device(): lax.dot_general(lax.all_gather(lower_panel, 'col', axis=0, tiled=True), t...]
    another operation x29 -> x0, local copies, waits for them, and re-layouts: 23.4 us -> none
    another operation x15 -> x0, matrix products: 13 us -> none  [per_device(): jax.scipy.linalg.solve_triangular(block_full, right_side, trans=1, lower=...]
  transfers between devices with their start and end apart: 3 -> 0, of which waited for: 2 -> 0; matrix products, arithmetic and copies ran while one was open for 40% -> 0% of each run, Pallas kernels for 0% -> 0%
where the time goes in v2:
time: 128 us
  Pallas kernels  126 us (98%)
  local copies, waits for them, and re-layouts  1.57 us (1%)
    pallas_call x1, Pallas kernels, per_device(): pl.pallas_call(kernel, name='window_solve', out_shape=jax.ShapeDtypeStruc...  126 us

profile of v2, /device:TPU:1, one launch (start us, length us, event | category | flops | bytes accessed | tf_op | source)
XLA Modules:
  0.0 127.7 jit_solution(18362476676312355129)
XLA Ops:
  0.0 126.2 %window_solve.1 = f32[128,256]{1,0:T(8,128)} custom-call(f32[4,4,504,256]{3,2,1,0:T(8,128)} %bitcast.1, f32[504,1024]{1,0:T(8,128)} %panel.1, f32[128,256]{1,0:T(8,128)} %rhs.1, f32[8,1024]{1,0:T(8,128)} %block.1), custom_call_target="tpu_custom_call" | custom-call | tf_op jit(solution)/shard_map/window_solve/pallas_call | solution.py:332
  126.2 1.6 %copy.6 = f32[128,256]{1,0:T(8,128)} copy(f32[128,256]{1,0:T(8,128)} %window_solve.1) | data formatting | bytes 262144

commit v3 on v2

--- a/solution.py
+++ b/solution.py
@@ -15,9 +15,9 @@
 COLS = 256
 BLK = 128
 QUARTER = 16
-CHUNKS = [(None, 0, 0), (None, 0, 1)] + [(p, d, h) for h in range(2) for d in (1, 3, 2) for p in range(2)]
+CHUNKS = [(None, 0, 0), (None, 0, 1)] + [(p, d, h) for near in ((1, 3), (2,)) for h in range(2) for d in near for p in range(2)]
 NUMBER = {chunk: q for q, chunk in enumerate(CHUNKS)}
-COPIES = 112
+COPIES = 128
 
 
 def split(value):
@@ -35,7 +35,7 @@
 
 def kernel(
     tail, panel, rhs, block, out,
-    tbuf, lbuf, lsplit, tt, cbuf, wrow, gfull, gsplit, rhs_in,
+    tbuf, fwd, lbuf, lsplit, tt, cbuf, wrow, gfull, gsplit, rhs_in,
     r1, part, ring, psum, r3, xs, obuf,
     send_sem, recv_sem, local_sem,
 ):
@@ -139,11 +139,26 @@
         at = lbuf.at[p, above, half(p, 1), :]
         onward.append(copy(at, at, across(p, 3)))
 
-    pieces = {}
+    pieces, hops, far = {}, {}, {}
+    for p, d, h in CHUNKS[2:10]:
+        pieces[p, d, h] = copy(piece(p, d, h), landing(p, d, h), along(p, d))
     for h in range(2):
-        for d in (1, 3, 2):
+        for i in range(2):
             for p in range(2):
-                pieces[p, d, h] = copy(piece(p, d, h), landing(p, d, h), along(p, d))
+                side, columns = pl.ds(2 * i, 2), pl.ds(h * BLK, BLK)
+                if p == 0:
+                    src = tail.at[side, (y + 2) % 4, pl.ds(0, LEN[0]), columns]
+                else:
+                    src = tail.at[(z + 2) % 4, side, pl.ds(LEN[0], LEN[1]), columns]
+                dst = fwd.at[p, h, i, :, pl.ds(0, LEN[p]), :]
+                hops[p, h, i] = copy(src, dst, along(p, 1 + 2 * i))
+
+    def relay(p, h):
+        for i in range(2):
+            hops[p, h, i].wait_recv()
+            src = fwd.at[p, h, i, :, pl.ds(0, LEN[p]), :]
+            dst = tbuf.at[p, 2, h, pl.ds(2 * i, 2), pl.ds(0, LEN[p]), :]
+            far[p, h, i] = copy(src, dst, along(p, 1 + 2 * i))
 
     for made in over_z:
         made.wait_recv()
@@ -167,39 +182,57 @@
     over_x = [copy(gfull.at[row], gfull.at[row], where(dx=i)) for i in (1, 3, 2)]
     to_other = [copy(gfull.at[row], gfull.at[row], where(dc=1))]
 
-    for made in own_panel:
-        made.wait()
-    for up, down in second:
-        up.wait_recv()
-        down.wait_recv()
-    for made in onward:
-        made.wait_recv()
-
-    @pl.loop(0, 2)
-    def _(p):
-        @pl.loop(0, 8)
+    def split_panel(p, slot):
+        @pl.loop(0, 2)
         def _(step):
-            high, low = split(lbuf[p, step // 2, aligned((step % 2) * BLK, BLK, BLK), :])
-            lsplit[p, aligned(step * BLK, BLK, BLK), :] = low
-            lsplit[p, aligned(DEEP + step * BLK, BLK, BLK), :] = high
-
-    def product(p, sources, store):
-        for i, (d, h) in enumerate(sources):
-
-            @pl.loop(0, 4)
-            def _(step):
-                high, low = split(tbuf[p, d, h, step].T)
-                tt[pl.ds(i * BLK, BLK), aligned(step * PART, PART, PART)] = high
-                tt[pl.ds(i * BLK, BLK), aligned(DEEP + step * PART, PART, PART)] = low
-
-        height = pl.ds(0, len(sources) * BLK)
+            high, low = split(lbuf[p, slot, aligned(step * BLK, BLK, BLK), :])
+            lsplit[p, aligned(slot * PART + step * BLK, BLK, BLK), :] = low
+            lsplit[p, aligned(DEEP + slot * PART + step * BLK, BLK, BLK), :] = high
+
+    def turn(p, i, d, h, slots):
+        @pl.loop(*slots)
+        def _(step):
+            high, low = split(tbuf[p, d, h, step].T)
+            tt[p, pl.ds(i * BLK, BLK), aligned(step * PART, PART, PART)] = high
+            tt[p, pl.ds(i * BLK, BLK), aligned(DEEP + step * PART, PART, PART)] = low
+
+    def add_own(p, slot):
+        high_at, low_at = aligned(slot * PART, PART, PART), aligned(DEEP + slot * PART, PART, PART)
 
         @pl.loop(0, 4)
         def _(step):
             at = aligned(step * 256, 256, 256)
-            value = dot(tt[height, :], lsplit[p, :, at]) + dot(tt[height, :DEEP], lsplit[p, DEEP:, at])
-            for i in range(len(sources)):
-                store(i, at, value[i * BLK : (i + 1) * BLK])
+            value = dot(tt[p, :, low_at], lsplit[p, low_at, at]) + dot(tt[p, :, high_at], lsplit[p, high_at, at])
+            value += dot(tt[p, :, high_at], lsplit[p, low_at, at])
+            cbuf[0, :, at] += value[:BLK]
+            cbuf[1, :, at] += value[BLK:]
+
+    for made in own_panel + own_tail:
+        made.wait()
+    own_rhs.wait()
+    turned = rhs_in[...].T
+    for h in range(2):
+        cbuf[h] = jnp.zeros((BLK, WIN), F32)
+        cbuf[h, :, own_cols] = -turned[h * BLK : (h + 1) * BLK]
+    for p in range(2):
+        split_panel(p, place[p])
+        for h in range(2):
+            turn(p, h, 0, h, (0, 4))
+    for p in (1, 0):
+        for made in second[1 - p]:
+            made.wait_recv()
+        split_panel(p, (place[p] + 3) % 4)
+        split_panel(p, (place[p] + 1) % 4)
+
+        @pl.loop(0, 3)
+        def _(i):
+            add_own(p, (place[p] + 3 + i) % 4)
+
+    for p in (1, 0):
+        for made in onward[2 * (1 - p) : 2 * (1 - p) + 2]:
+            made.wait_recv()
+        split_panel(p, (place[p] + 2) % 4)
+        add_own(p, (place[p] + 2) % 4)
 
     keep, give = aligned(core * 64, 64, 64), aligned((1 - core) * 64, 64, 64)
     pair, ringed, third = {}, {}, {}
@@ -216,50 +249,68 @@
         for made in ringed[q]:
             made.wait_recv()
         psum[q] = part[q, x] + ring[q, 0] + ring[q, 1] + ring[q, 2]
+
+    def to_owner(q):
         p, d, _ = CHUNKS[q]
-        if d:
-            third[q] = copy(psum.at[q], r3.at[q - 2], along(p, -d))
-
-    def chunk_product(p, sources):
-        numbers = [NUMBER[p, d, h] for d, h in sources]
-        for d, h in sources:
-            pieces[p, d, h].wait_recv()
-
-        def store(i, at, value):
-            cbuf[numbers[i], :, at] = value
-
-        product(p, sources, store)
+        third[q] = copy(psum.at[q], r3.at[q - 2], along(p, -d))
+
+    def near_product(p, h):
+        for i, d in enumerate((1, 3)):
+            turn(p, i, d, h, (0, 4))
+        numbers = NUMBER[p, 1, h], NUMBER[p, 3, h]
+
+        @pl.loop(0, 4)
+        def _(step):
+            at = aligned(step * 256, 256, 256)
+            value = dot(tt[p], lsplit[p, :, at]) + dot(tt[p, :, :DEEP], lsplit[p, DEEP:, at])
+            for i, q in enumerate(numbers):
+                cbuf[q, :, at] = value[i * BLK : (i + 1) * BLK]
+
         for q in numbers:
             to_pair(q)
-        return numbers
-
-    def store_own(i, at, value):
-        cbuf[i, :, at] = value
-
-    def add_own(i, at, value):
-        cbuf[i, :, at] += value
-
-    for made in own_tail:
-        made.wait()
-    product(0, [(0, 0), (0, 1)], store_own)
-    product(1, [(0, 0), (0, 1)], add_own)
-    own_rhs.wait()
-    turned = rhs_in[...].T
-    for h in range(2):
-        cbuf[h, :, own_cols] += -turned[h * BLK : (h + 1) * BLK]
-        to_pair(h)
+
+    def far_product(p, h):
+        for i in range(2):
+            far[p, h, i].wait_recv()
+        turn(p, 0, 2, h, (0, 4))
+        q = NUMBER[p, 2, h]
+
+        @pl.loop(0, 4)
+        def _(step):
+            at = aligned(step * 256, 256, 256)
+            value = dot(tt[p, :BLK, :], lsplit[p, :, at]) + dot(tt[p, :BLK, :DEEP], lsplit[p, DEEP:, at])
+            cbuf[q, :, at] = value
+
+        to_pair(q)
+
+    def near_arrived(p, h):
+        for d in (1, 3):
+            pieces[p, d, h].wait_recv()
+
+    to_pair(0)
+    to_pair(1)
+    near_arrived(0, 0)
+    near_product(0, 0)
+    to_ring(0)
+    to_ring(1)
     for made, i in zip(over_x, (1, 3, 2)):
         made.wait_recv()
         slot = 2 * ((x - i + 4) % 4) + core
         to_other.append(copy(gfull.at[slot], gfull.at[slot], where(dc=1)))
-    to_ring(0)
-    to_ring(1)
-
-    a = chunk_product(0, [(1, 0), (3, 0)])
-    b = chunk_product(1, [(1, 0), (3, 0)])
-    for q in a + b:
+    near_arrived(1, 0)
+    near_product(1, 0)
+    for q in (2, 4, 3, 5):
         to_ring(q)
-
+    near_arrived(0, 1)
+    near_product(0, 1)
+    near_arrived(1, 1)
+    near_product(1, 1)
+    relay(0, 0)
+    relay(1, 0)
+    for q in (6, 8, 7, 9):
+        to_ring(q)
+    from_ring(0)
+    from_ring(1)
     for made in to_other:
         made.wait_recv()
 
@@ -269,30 +320,29 @@
         gsplit[0, step] = high
         gsplit[1, step] = low
 
-    from_ring(0)
-    from_ring(1)
-    c = chunk_product(0, [(2, 0)]) + chunk_product(1, [(2, 0)])
-    for q in a + b:
+    relay(0, 1)
+    relay(1, 1)
+    for q in (2, 4, 3, 5):
         from_ring(q)
-    for q in c:
-        to_ring(q)
-    a = chunk_product(0, [(1, 1), (3, 1)])
-    b = chunk_product(1, [(1, 1), (3, 1)])
-    for q in c:
+    for p in range(2):
+        far_product(p, 0)
+    for q in (6, 8, 7, 9):
         from_ring(q)
-    for q in a + b:
-        to_ring(q)
-    c = chunk_product(0, [(2, 1)])
-    for q in a + b:
+    to_ring(10)
+    to_ring(11)
+    far_product(0, 1)
+    for q in (2, 4, 6, 8):
+        to_owner(q)
+    to_ring(12)
+    far_product(1, 1)
+    for q in (3, 5, 7, 9):
+        to_owner(q)
+    to_ring(13)
+    for q in (10, 11, 12, 13):
         from_ring(q)
-    c += chunk_product(1, [(2, 1)])
-    for q in c:
-        to_ring(q)
+        to_owner(q)
     totals = []
     for h in range(2):
-        if h:
-            for q in c:
-                from_ring(q)
         total = psum[h]
         for d in (1, 3, 2):
             for p in range(2):
@@ -337,9 +387,10 @@
         out_specs=pl.BlockSpec(memory_space=pltpu.VMEM),
         scratch_shapes=[
             pltpu.VMEM((2, 4, 2, 4, PART, BLK), F32),
+            pltpu.VMEM((2, 2, 2, 2, PART, BLK), F32),
             pltpu.VMEM((2, 4, PART, WIN), F32),
             pltpu.VMEM((2, 2 * DEEP, WIN), BF16),
-            pltpu.VMEM((COLS, 2 * DEEP), BF16),
+            pltpu.VMEM((2, COLS, 2 * DEEP), BF16),
             pltpu.VMEM((count, BLK, WIN), F32),
             pltpu.VMEM((BLK, WIN), F32),
             pltpu.VMEM((8, BLK, WIN), F32),

time: 128 us -> 118 us (0.922)
  Pallas kernels: 126 us -> 116 us
    pallas_call x1, Pallas kernels: 126 us -> 116 us  [per_device(): pl.pallas_call(kernel, name='window_solve', out_shape=jax.ShapeDtypeStruc...]
where the time goes in v3:
time: 118 us; the launch traced here: 117 us
  Pallas kernels  116 us (98%)
  local copies, waits for them, and re-layouts  1.57 us (1%)
    pallas_call x1, Pallas kernels, per_device(): pl.pallas_call(kernel, name='window_solve', out_shape=jax.ShapeDtypeStruc...  116 us

profile of v3, /device:TPU:1, one launch (start us, length us, event | category | flops | bytes accessed | tf_op | source)
XLA Modules:
  0.0 117.4 jit_solution(13028642477345950745)
XLA Ops:
  0.0 115.9 %window_solve.1 = f32[128,256]{1,0:T(8,128)} custom-call(f32[4,4,504,256]{3,2,1,0:T(8,128)} %bitcast.1, f32[504,1024]{1,0:T(8,128)} %panel.1, f32[128,256]{1,0:T(8,128)} %rhs.1, f32[8,1024]{1,0:T(8,128)} %block.1), custom_call_target="tpu_custom_call" | custom-call | tf_op jit(solution)/shard_map/window_solve/pallas_call | solution.py:382
  115.9 1.6 %copy.6 = f32[128,256]{1,0:T(8,128)} copy(f32[128,256]{1,0:T(8,128)} %window_solve.1) | data formatting | bytes 262144

commit v4 on v3

--- a/solution.py
+++ b/solution.py
@@ -17,7 +17,8 @@
 QUARTER = 16
 CHUNKS = [(None, 0, 0), (None, 0, 1)] + [(p, d, h) for near in ((1, 3), (2,)) for h in range(2) for d in near for p in range(2)]
 NUMBER = {chunk: q for q, chunk in enumerate(CHUNKS)}
-COPIES = 128
+SLOT = (0, 1, 3, 2)
+RECEIVED, SENDING, LOCAL = 62, 15, 8
 
 
 def split(value):
@@ -42,8 +43,6 @@
     row, col = lax.axis_index("row"), lax.axis_index("col")
     x, core = row // 2, row % 2
     z, y = col // 4, col % 4
-    counter = [0]
-    started = []
 
     def where(dx=0, dc=0, dz=0, dy=0):
         new_row = 2 * ((x + dx + 4) % 4) + (core + dc) % 2
@@ -58,20 +57,24 @@
 
     place = (z, y)
 
-    def copy(src, dst, target):
-        index = counter[0]
-        counter[0] += 1
-        made = pltpu.make_async_remote_copy(
+    received, sending = {}, {}
+
+    def copy(src, dst, target, group, sent):
+        at, out_at = received.setdefault(group, len(received)), sending.setdefault(sent, len(sending))
+        pltpu.make_async_remote_copy(
             src_ref=src,
             dst_ref=dst,
-            send_sem=send_sem.at[index],
-            recv_sem=recv_sem.at[index],
+            send_sem=send_sem.at[out_at],
+            recv_sem=recv_sem.at[at],
             device_id=target,
             device_id_type=pl.DeviceIdType.MESH,
-        )
-        made.start()
-        started.append(made)
-        return made
+        ).start()
+
+    def arrived(group, ref):
+        pltpu.make_async_copy(ref, ref, recv_sem.at[received[group]]).wait()
+
+    def gone(sent, ref):
+        pltpu.make_async_copy(ref, ref, send_sem.at[sending[sent]]).wait()
 
     local = []
 
@@ -88,7 +91,7 @@
         return tail.at[(z + step) % 4, :, pl.ds(LEN[0], LEN[1]), columns]
 
     def landing(p, d, h):
-        return tbuf.at[p, d, h, :, pl.ds(0, LEN[p]), :]
+        return tbuf.at[p, SLOT[d], h, :, pl.ds(0, LEN[p]), :]
 
     partners = [where(dy=i) for i in (1, 2, 3)] + [where(dz=i) for i in (1, 2, 3)]
     partners += [where(dx=i, dc=j) for i in range(4) for j in range(2) if (i, j) != (0, 0)]
@@ -97,24 +100,27 @@
         pl.semaphore_signal(barrier, inc=1, device_id=partner, device_id_type=pl.DeviceIdType.MESH)
     pl.semaphore_wait(barrier, len(partners))
 
-    mine = aligned(col * 8, 8, 8)
-    over_y = [copy(block, wrow.at[mine, :], where(dy=i)) for i in (1, 3, 2)]
+    lanes = pl.ds(0, WIN // 2), pl.ds(WIN // 2, WIN // 2)
+    for i in (1, 3, 2):
+        for p in range(2):
+            copy(block.at[:, lanes[p]], wrow.at[z, y, :, lanes[p]], along(p, i), "shards", "shards")
 
     def half(p, side):
         return pl.ds(0, 128) if side == 0 else pl.ds(128, LEN[p] - 128)
 
-    def send_panel(p, step, side):
+    def send_panel(p, step, side, group):
         src = pl.ds(p * PART + half(p, side).start, half(p, side).size)
-        return copy(panel.at[src, :], lbuf.at[p, place[p], half(p, side), :], across(p, step))
-
-    first = [(send_panel(p, 1, 0), send_panel(p, 3, 1)) for p in (1, 0)]
-    own_block = bring(block, wrow.at[mine, :])
+        copy(panel.at[src, :], lbuf.at[p, place[p], half(p, side), :], across(p, step), group, ("panel", p))
+
+    for p in (1, 0):
+        send_panel(p, 1, 0, ("up", p))
+        send_panel(p, 3, 1, ("down", p))
+    own_block = bring(block, wrow.at[z, y])
     own_panel = [
         bring(panel.at[pl.ds(p * PART, LEN[p]), :], lbuf.at[p, place[p], pl.ds(0, LEN[p]), :]) for p in range(2)
     ]
     own_rhs = bring(rhs, rhs_in)
     own_tail = [bring(piece(p, 0, h), landing(p, 0, h)) for p in range(2) for h in range(2)]
-    second = [(send_panel(1, 1, 1), send_panel(1, 3, 0))]
 
     for i in range(4):
         lbuf[1, i, LEN[1] :, :] = jnp.zeros((PART - LEN[1], WIN), F32)
@@ -123,25 +129,24 @@
                 tbuf[1, d, h, i, LEN[1] :, :] = jnp.zeros((PART - LEN[1], BLK), F32)
 
     own_block.wait()
-    for made in over_y:
-        made.wait_recv()
-    quarter = aligned(z * 32, 32, 32)
-    over_z = [copy(wrow.at[quarter, :], wrow.at[quarter, :], where(dz=i)) for i in (1, 3, 2)]
-    second.append((send_panel(0, 1, 1), send_panel(0, 3, 0)))
-
-    onward = []
-    for p, (up, down) in zip((1, 0), first):
-        below, above = (place[p] + 3) % 4, (place[p] + 1) % 4
-        up.wait_recv()
-        at = lbuf.at[p, below, half(p, 0), :]
-        onward.append(copy(at, at, across(p, 1)))
-        down.wait_recv()
-        at = lbuf.at[p, above, half(p, 1), :]
-        onward.append(copy(at, at, across(p, 3)))
-
-    pieces, hops, far = {}, {}, {}
+    arrived("shards", wrow.at[0, pl.ds(0, 3)])
+    for i in (1, 3, 2):
+        at = wrow.at[z, :, :, lanes[0]]
+        copy(at, at, where(dz=i), "rows", "rows")
+        at = wrow.at[:, y, :, lanes[1]]
+        copy(at, at, where(dy=i), "rows", "rows")
+    for p in (1, 0):
+        send_panel(p, 1, 1, ("second", p))
+        send_panel(p, 3, 0, ("second", p))
+
+    for p in (1, 0):
+        for name, step, side in (("up", 1, 0), ("down", 3, 1)):
+            at = lbuf.at[p, (place[p] - step + 4) % 4, half(p, side), :]
+            arrived((name, p), at)
+            copy(at, at, across(p, step), ("onward", p), ("panel", p))
+
     for p, d, h in CHUNKS[2:10]:
-        pieces[p, d, h] = copy(piece(p, d, h), landing(p, d, h), along(p, d))
+        copy(piece(p, d, h), landing(p, d, h), along(p, d), ("near", p, h), ("near", p))
     for h in range(2):
         for i in range(2):
             for p in range(2):
@@ -151,23 +156,22 @@
                 else:
                     src = tail.at[(z + 2) % 4, side, pl.ds(LEN[0], LEN[1]), columns]
                 dst = fwd.at[p, h, i, :, pl.ds(0, LEN[p]), :]
-                hops[p, h, i] = copy(src, dst, along(p, 1 + 2 * i))
+                copy(src, dst, along(p, 1 + 2 * i), ("hop", p, h), ("hop", p))
 
     def relay(p, h):
+        arrived(("hop", p, h), fwd.at[p, h, :, :, pl.ds(0, LEN[p]), :])
         for i in range(2):
-            hops[p, h, i].wait_recv()
             src = fwd.at[p, h, i, :, pl.ds(0, LEN[p]), :]
-            dst = tbuf.at[p, 2, h, pl.ds(2 * i, 2), pl.ds(0, LEN[p]), :]
-            far[p, h, i] = copy(src, dst, along(p, 1 + 2 * i))
-
-    for made in over_z:
-        made.wait_recv()
+            dst = tbuf.at[p, SLOT[2], h, pl.ds(2 * i, 2), pl.ds(0, LEN[p]), :]
+            copy(src, dst, along(p, 1 + 2 * i), ("far", p, h), ("far", p))
+
+    arrived("rows", wrow.at[pl.ds(0, 3)])
 
     rows = lax.broadcasted_iota(jnp.int32, (BLK, BLK), 0)
     cols = lax.broadcasted_iota(jnp.int32, (BLK, BLK), 1)
     eye = jnp.where(rows == cols, 1.0, 0.0).astype(F32)
     own_cols = aligned(row * BLK, BLK, BLK)
-    diagonal = wrow[:, own_cols]
+    diagonal = wrow[:, :, :, own_cols].reshape(BLK, BLK)
     on_diag = jnp.where(rows == cols, diagonal, 0.0)
     diag_rows = jnp.sum(on_diag, axis=1, keepdims=True)
     diag_cols = jnp.sum(on_diag, axis=0, keepdims=True)
@@ -177,10 +181,11 @@
         both = dot(jnp.concatenate([inverse, power], axis=0), power, HIGHEST)
         inverse, power = inverse + both[:BLK], both[BLK:]
     inverse = inverse / diag_cols
-    gfull[row] = dot(inverse, wrow[...], HIGHEST)
+    gfull[row] = dot(inverse, wrow[...].reshape(BLK, WIN), HIGHEST)
     gfull[row, :, own_cols] = inverse
-    over_x = [copy(gfull.at[row], gfull.at[row], where(dx=i)) for i in (1, 3, 2)]
-    to_other = [copy(gfull.at[row], gfull.at[row], where(dc=1))]
+    for i in (1, 3, 2):
+        copy(gfull.at[row], gfull.at[row], where(dx=i), "over_x", "blocks")
+    copy(gfull.at[row], gfull.at[row], where(dc=1), "to_other", "blocks")
 
     def split_panel(p, slot):
         @pl.loop(0, 2)
@@ -192,7 +197,7 @@
     def turn(p, i, d, h, slots):
         @pl.loop(*slots)
         def _(step):
-            high, low = split(tbuf[p, d, h, step].T)
+            high, low = split(tbuf[p, SLOT[d], h, step].T)
             tt[p, pl.ds(i * BLK, BLK), aligned(step * PART, PART, PART)] = high
             tt[p, pl.ds(i * BLK, BLK), aligned(DEEP + step * PART, PART, PART)] = low
 
@@ -219,8 +224,7 @@
         for h in range(2):
             turn(p, h, 0, h, (0, 4))
     for p in (1, 0):
-        for made in second[1 - p]:
-            made.wait_recv()
+        arrived(("second", p), lbuf.at[p, 0, pl.ds(0, LEN[p]), :])
         split_panel(p, (place[p] + 3) % 4)
         split_panel(p, (place[p] + 1) % 4)
 
@@ -229,30 +233,28 @@
             add_own(p, (place[p] + 3 + i) % 4)
 
     for p in (1, 0):
-        for made in onward[2 * (1 - p) : 2 * (1 - p) + 2]:
-            made.wait_recv()
+        arrived(("onward", p), lbuf.at[p, 0, pl.ds(0, LEN[p]), :])
         split_panel(p, (place[p] + 2) % 4)
         add_own(p, (place[p] + 2) % 4)
 
     keep, give = aligned(core * 64, 64, 64), aligned((1 - core) * 64, 64, 64)
-    pair, ringed, third = {}, {}, {}
 
     def to_pair(q):
-        pair[q] = copy(cbuf.at[q, give, :], r1.at[q], where(dc=1))
+        copy(cbuf.at[q, give, :], r1.at[q], where(dc=1), ("pair", q), "pair")
 
     def to_ring(q):
-        pair[q].wait_recv()
+        arrived(("pair", q), r1.at[q])
         part[q] = (cbuf[q, keep, :] + r1[q]).reshape(4, QUARTER, WIN)
-        ringed[q] = [copy(part.at[q, (x + i) % 4], ring.at[q, i - 1], where(dx=i)) for i in (2, 1, 3)]
+        for i in (2, 1, 3):
+            copy(part.at[q, (x + i) % 4], ring.at[q, i - 1], where(dx=i), ("ring", q), "ring")
 
     def from_ring(q):
-        for made in ringed[q]:
-            made.wait_recv()
+        arrived(("ring", q), ring.at[q])
         psum[q] = part[q, x] + ring[q, 0] + ring[q, 1] + ring[q, 2]
 
     def to_owner(q):
         p, d, _ = CHUNKS[q]
-        third[q] = copy(psum.at[q], r3.at[q - 2], along(p, -d))
+        copy(psum.at[q], r3.at[q - 2], along(p, -d), "owner", "owner")
 
     def near_product(p, h):
         for i, d in enumerate((1, 3)):
@@ -269,34 +271,48 @@
         for q in numbers:
             to_pair(q)
 
-    def far_product(p, h):
-        for i in range(2):
-            far[p, h, i].wait_recv()
-        turn(p, 0, 2, h, (0, 4))
+    def far_product(p, h, s):
+        if s:
+            arrived(("far", p, h), landing(p, 2, h))
+            turn(p, 0, 2, h, (0, 4))
         q = NUMBER[p, 2, h]
 
-        @pl.loop(0, 4)
+        @pl.loop(2 * s, 2 * s + 2)
         def _(step):
             at = aligned(step * 256, 256, 256)
             value = dot(tt[p, :BLK, :], lsplit[p, :, at]) + dot(tt[p, :BLK, :DEEP], lsplit[p, DEEP:, at])
             cbuf[q, :, at] = value
 
-        to_pair(q)
+        copy(cbuf.at[q, give, lanes[s]], r1.at[q, :, lanes[s]], where(dc=1), ("pair", q, s), "pair")
+
+    def to_ring_half(q, s):
+        arrived(("pair", q, s), r1.at[q, :, lanes[s]])
+        value = cbuf[q, keep, lanes[s]] + r1[q, :, lanes[s]]
+        part[q, :, :, lanes[s]] = value.reshape(4, QUARTER, WIN // 2)
+        for i in (2, 1, 3):
+            src, dst = part.at[q, (x + i) % 4, :, lanes[s]], ring.at[q, i - 1, :, lanes[s]]
+            copy(src, dst, where(dx=i), ("ring", q, s), "ring")
+
+    def from_ring_half(q, s):
+        at = lanes[s]
+        arrived(("ring", q, s), ring.at[q, :, :, at])
+        psum[q, :, at] = part[q, x, :, at] + ring[q, 0, :, at] + ring[q, 1, :, at] + ring[q, 2, :, at]
+        p, d, _ = CHUNKS[q]
+        copy(psum.at[q, :, at], r3.at[q - 2, :, at], along(p, -d), "owner", "owner")
 
     def near_arrived(p, h):
-        for d in (1, 3):
-            pieces[p, d, h].wait_recv()
+        arrived(("near", p, h), tbuf.at[p, pl.ds(1, 2), h, :, pl.ds(0, LEN[p]), :])
 
     to_pair(0)
     to_pair(1)
+    to_ring(0)
+    to_ring(1)
     near_arrived(0, 0)
     near_product(0, 0)
-    to_ring(0)
-    to_ring(1)
-    for made, i in zip(over_x, (1, 3, 2)):
-        made.wait_recv()
+    arrived("over_x", gfull.at[pl.ds(0, 3)])
+    for i in (1, 3, 2):
         slot = 2 * ((x - i + 4) % 4) + core
-        to_other.append(copy(gfull.at[slot], gfull.at[slot], where(dc=1)))
+        copy(gfull.at[slot], gfull.at[slot], where(dc=1), "to_other", "blocks")
     near_arrived(1, 0)
     near_product(1, 0)
     for q in (2, 4, 3, 5):
@@ -311,8 +327,7 @@
         to_ring(q)
     from_ring(0)
     from_ring(1)
-    for made in to_other:
-        made.wait_recv()
+    arrived("to_other", gfull.at[pl.ds(0, 4)])
 
     @pl.loop(0, 8)
     def _(step):
@@ -324,30 +339,38 @@
     relay(1, 1)
     for q in (2, 4, 3, 5):
         from_ring(q)
-    for p in range(2):
-        far_product(p, 0)
+    far_product(0, 0, 1)
+    far_product(0, 0, 0)
+    far_product(1, 0, 1)
+    to_ring_half(10, 1)
+    far_product(1, 0, 0)
+    to_ring_half(10, 0)
+    to_ring_half(11, 1)
+    to_ring_half(11, 0)
     for q in (6, 8, 7, 9):
         from_ring(q)
-    to_ring(10)
-    to_ring(11)
-    far_product(0, 1)
+    far_product(0, 1, 1)
+    far_product(0, 1, 0)
     for q in (2, 4, 6, 8):
         to_owner(q)
-    to_ring(12)
-    far_product(1, 1)
+    to_ring_half(12, 1)
+    far_product(1, 1, 1)
+    to_ring_half(12, 0)
+    far_product(1, 1, 0)
     for q in (3, 5, 7, 9):
         to_owner(q)
-    to_ring(13)
+    to_ring_half(13, 1)
+    to_ring_half(13, 0)
     for q in (10, 11, 12, 13):
-        from_ring(q)
-        to_owner(q)
+        for s in (1, 0):
+            from_ring_half(q, s)
+    arrived("owner", r3)
     totals = []
     for h in range(2):
         total = psum[h]
         for d in (1, 3, 2):
             for p in range(2):
                 q = NUMBER[p, d, h]
-                third[q].wait_recv()
                 total += r3[q - 2]
         totals.append(total)
 
@@ -363,17 +386,26 @@
 
     own = aligned(core * 64 + x * QUARTER, QUARTER, QUARTER)
     obuf[:, own, :] = xs[row]
-    spread = []
     for i in range(4):
         for j in range(2):
             if (i, j) != (0, 0):
                 target = where(dx=i, dc=j)
-                spread.append(copy(xs.at[target[0]], obuf.at[:, own, :], target))
-    for made in spread:
-        made.wait_recv()
+                copy(xs.at[target[0]], obuf.at[:, own, :], target, "spread", "spread")
+    arrived("spread", xs.at[pl.ds(0, 7)])
     out[...] = obuf[...].reshape(COLS, BLK).T
-    for made in started:
-        made.wait_send()
+    gone("shards", wrow.at[0, pl.ds(0, 3)])
+    gone("rows", wrow.at[pl.ds(0, 3)])
+    gone("blocks", gfull.at[pl.ds(0, 7)])
+    for p in range(2):
+        gone(("panel", p), lbuf.at[p, pl.ds(0, 3), pl.ds(0, LEN[p]), :])
+        gone(("near", p), tbuf.at[p, pl.ds(1, 2), :, :, pl.ds(0, LEN[p]), :])
+        gone(("hop", p), fwd.at[p, :, :, :, pl.ds(0, LEN[p]), :])
+        gone(("far", p), tbuf.at[p, SLOT[2], :, :, pl.ds(0, LEN[p]), :])
+    gone("pair", r1)
+    gone("ring", ring)
+    gone("owner", r3)
+    gone("spread", xs.at[pl.ds(0, 7)])
+    assert len(received) == RECEIVED and len(sending) == SENDING
 
 
 def per_device(tail_vectors, lower_panel, window_rhs, window_block):
@@ -392,7 +424,7 @@
             pltpu.VMEM((2, 2 * DEEP, WIN), BF16),
             pltpu.VMEM((2, COLS, 2 * DEEP), BF16),
             pltpu.VMEM((count, BLK, WIN), F32),
-            pltpu.VMEM((BLK, WIN), F32),
+            pltpu.VMEM((4, 4, 8, WIN), F32),
             pltpu.VMEM((8, BLK, WIN), F32),
             pltpu.VMEM((2, 8, BLK, WIN), BF16),
             pltpu.VMEM((BLK, COLS), F32),
@@ -403,9 +435,9 @@
             pltpu.VMEM((count - 2, QUARTER, WIN), F32),
             pltpu.VMEM((8, 2, QUARTER, BLK), F32),
             pltpu.VMEM((2, BLK, BLK), F32),
-            pltpu.SemaphoreType.DMA((COPIES,)),
-            pltpu.SemaphoreType.DMA((COPIES,)),
-            pltpu.SemaphoreType.DMA((8,)),
+            pltpu.SemaphoreType.DMA((SENDING,)),
+            pltpu.SemaphoreType.DMA((RECEIVED,)),
+            pltpu.SemaphoreType.DMA((LOCAL,)),
         ],
         compiler_params=pltpu.CompilerParams(
             collective_id=0, has_side_effects=True, vmem_limit_bytes=62 * 1024 * 1024

time: 118 us -> 115 us (0.975)
  Pallas kernels: 116 us -> 113 us
    pallas_call x1, Pallas kernels: 116 us -> 113 us  [per_device(): pl.pallas_call(kernel, name='window_solve', out_shape=jax.ShapeDtypeStruc...]
where the time goes in v4:
time: 115 us
  Pallas kernels  113 us (98%)
  local copies, waits for them, and re-layouts  1.57 us (1%)
    pallas_call x1, Pallas kernels, per_device(): pl.pallas_call(kernel, name='window_solve', out_shape=jax.ShapeDtypeStruc...  113 us

profile of v4, /device:TPU:1, one launch (start us, length us, event | category | flops | bytes accessed | tf_op | source)
XLA Modules:
  0.0 114.9 jit_solution(5868804353287318440)
XLA Ops:
  0.0 113.3 %window_solve.1 = f32[128,256]{1,0:T(8,128)} custom-call(f32[4,4,504,256]{3,2,1,0:T(8,128)} %bitcast.1, f32[504,1024]{1,0:T(8,128)} %panel.1, f32[128,256]{1,0:T(8,128)} %rhs.1, f32[8,1024]{1,0:T(8,128)} %block.1), custom_call_target="tpu_custom_call" | custom-call | tf_op jit(solution)/shard_map/window_solve/pallas_call | solution.py:414
  113.3 1.6 %copy.6 = f32[128,256]{1,0:T(8,128)} copy(f32[128,256]{1,0:T(8,128)} %window_solve.1) | data formatting | bytes 262144

commit v5 on v4

--- a/solution.py
+++ b/solution.py
@@ -15,7 +15,7 @@
 COLS = 256
 BLK = 128
 QUARTER = 16
-CHUNKS = [(None, 0, 0), (None, 0, 1)] + [(p, d, h) for near in ((1, 3), (2,)) for h in range(2) for d in near for p in range(2)]
+CHUNKS = [(None, 0, 0), (None, 0, 1)] + [(p, d, h) for near in ((1, 3), (2,)) for h in range(2) for p in range(2) for d in near]
 NUMBER = {chunk: q for q, chunk in enumerate(CHUNKS)}
 SLOT = (0, 1, 3, 2)
 RECEIVED, SENDING, LOCAL = 62, 15, 8
@@ -102,8 +102,7 @@
 
     lanes = pl.ds(0, WIN // 2), pl.ds(WIN // 2, WIN // 2)
     for i in (1, 3, 2):
-        for p in range(2):
-            copy(block.at[:, lanes[p]], wrow.at[z, y, :, lanes[p]], along(p, i), "shards", "shards")
+        copy(block, wrow.at[z, y], where(dy=i), "shards", "shards")
 
     def half(p, side):
         return pl.ds(0, 128) if side == 0 else pl.ds(128, LEN[p] - 128)
@@ -131,10 +130,7 @@
     own_block.wait()
     arrived("shards", wrow.at[0, pl.ds(0, 3)])
     for i in (1, 3, 2):
-        at = wrow.at[z, :, :, lanes[0]]
-        copy(at, at, where(dz=i), "rows", "rows")
-        at = wrow.at[:, y, :, lanes[1]]
-        copy(at, at, where(dy=i), "rows", "rows")
+        copy(wrow.at[z], wrow.at[z], where(dz=i), "rows", "rows")
     for p in (1, 0):
         send_panel(p, 1, 1, ("second", p))
         send_panel(p, 3, 0, ("second", p))
@@ -239,37 +235,44 @@
 
     keep, give = aligned(core * 64, 64, 64), aligned((1 - core) * 64, 64, 64)
 
-    def to_pair(q):
-        copy(cbuf.at[q, give, :], r1.at[q], where(dc=1), ("pair", q), "pair")
-
-    def to_ring(q):
-        arrived(("pair", q), r1.at[q])
-        part[q] = (cbuf[q, keep, :] + r1[q]).reshape(4, QUARTER, WIN)
+    def to_pair(q, n, s):
+        at = pl.ds(q, n)
+        copy(cbuf.at[at, give, lanes[s]], r1.at[at, :, lanes[s]], where(dc=1), ("pair", q, s), "pair")
+
+    def to_ring(q, n, s):
+        at = pl.ds(q, n)
+        arrived(("pair", q, s), r1.at[at, :, lanes[s]])
+        value = cbuf[at, keep, lanes[s]] + r1[at, :, lanes[s]]
+        part[at, :, :, lanes[s]] = value.reshape(n, 4, QUARTER, WIN // 2)
         for i in (2, 1, 3):
-            copy(part.at[q, (x + i) % 4], ring.at[q, i - 1], where(dx=i), ("ring", q), "ring")
-
-    def from_ring(q):
-        arrived(("ring", q), ring.at[q])
-        psum[q] = part[q, x] + ring[q, 0] + ring[q, 1] + ring[q, 2]
-
-    def to_owner(q):
+            src, dst = part.at[at, (x + i) % 4, :, lanes[s]], ring.at[at, i - 1, :, lanes[s]]
+            copy(src, dst, where(dx=i), ("ring", q, s), "ring")
+
+    def from_ring(q, n, s):
+        arrived(("ring", q, s), ring.at[pl.ds(q, n), :, :, lanes[s]])
+        at = lanes[s]
+        for k in range(q, q + n):
+            psum[k, :, at] = part[k, x, :, at] + ring[k, 0, :, at] + ring[k, 1, :, at] + ring[k, 2, :, at]
+
+    def to_owner(q, at=pl.ds(0, WIN)):
         p, d, _ = CHUNKS[q]
-        copy(psum.at[q], r3.at[q - 2], along(p, -d), "owner", "owner")
-
-    def near_product(p, h):
-        for i, d in enumerate((1, 3)):
-            turn(p, i, d, h, (0, 4))
-        numbers = NUMBER[p, 1, h], NUMBER[p, 3, h]
-
-        @pl.loop(0, 4)
+        copy(psum.at[q, :, at], r3.at[q - 2, :, at], along(p, -d), "owner", "owner")
+
+    def near_product(p, h, s):
+        if s:
+            arrived(("near", p, h), tbuf.at[p, pl.ds(1, 2), h, :, pl.ds(0, LEN[p]), :])
+            for i, d in enumerate((1, 3)):
+                turn(p, i, d, h, (0, 4))
+        q = NUMBER[p, 1, h]
+
+        @pl.loop(2 * s, 2 * s + 2)
         def _(step):
             at = aligned(step * 256, 256, 256)
             value = dot(tt[p], lsplit[p, :, at]) + dot(tt[p, :, :DEEP], lsplit[p, DEEP:, at])
-            for i, q in enumerate(numbers):
-                cbuf[q, :, at] = value[i * BLK : (i + 1) * BLK]
-
-        for q in numbers:
-            to_pair(q)
+            for i in range(2):
+                cbuf[q + i, :, at] = value[i * BLK : (i + 1) * BLK]
+
+        to_pair(q, 2, s)
 
     def far_product(p, h, s):
         if s:
@@ -283,50 +286,36 @@
             value = dot(tt[p, :BLK, :], lsplit[p, :, at]) + dot(tt[p, :BLK, :DEEP], lsplit[p, DEEP:, at])
             cbuf[q, :, at] = value
 
-        copy(cbuf.at[q, give, lanes[s]], r1.at[q, :, lanes[s]], where(dc=1), ("pair", q, s), "pair")
-
-    def to_ring_half(q, s):
-        arrived(("pair", q, s), r1.at[q, :, lanes[s]])
-        value = cbuf[q, keep, lanes[s]] + r1[q, :, lanes[s]]
-        part[q, :, :, lanes[s]] = value.reshape(4, QUARTER, WIN // 2)
-        for i in (2, 1, 3):
-            src, dst = part.at[q, (x + i) % 4, :, lanes[s]], ring.at[q, i - 1, :, lanes[s]]
-            copy(src, dst, where(dx=i), ("ring", q, s), "ring")
-
-    def from_ring_half(q, s):
-        at = lanes[s]
-        arrived(("ring", q, s), ring.at[q, :, :, at])
-        psum[q, :, at] = part[q, x, :, at] + ring[q, 0, :, at] + ring[q, 1, :, at] + ring[q, 2, :, at]
-        p, d, _ = CHUNKS[q]
-        copy(psum.at[q, :, at], r3.at[q - 2, :, at], along(p, -d), "owner", "owner")
-
-    def near_arrived(p, h):
-        arrived(("near", p, h), tbuf.at[p, pl.ds(1, 2), h, :, pl.ds(0, LEN[p]), :])
-
-    to_pair(0)
-    to_pair(1)
-    to_ring(0)
-    to_ring(1)
-    near_arrived(0, 0)
-    near_product(0, 0)
+        to_pair(q, 1, s)
+
+    to_pair(0, 2, 1)
+    to_pair(0, 2, 0)
+    to_ring(0, 2, 1)
+    to_ring(0, 2, 0)
+    near_product(0, 0, 1)
+    near_product(0, 0, 0)
+    to_ring(2, 2, 1)
+    near_product(1, 0, 1)
+    to_ring(2, 2, 0)
+    near_product(1, 0, 0)
+    to_ring(4, 2, 1)
     arrived("over_x", gfull.at[pl.ds(0, 3)])
     for i in (1, 3, 2):
         slot = 2 * ((x - i + 4) % 4) + core
         copy(gfull.at[slot], gfull.at[slot], where(dc=1), "to_other", "blocks")
-    near_arrived(1, 0)
-    near_product(1, 0)
-    for q in (2, 4, 3, 5):
-        to_ring(q)
-    near_arrived(0, 1)
-    near_product(0, 1)
-    near_arrived(1, 1)
-    near_product(1, 1)
+    to_ring(4, 2, 0)
+    from_ring(0, 2, 1)
+    from_ring(0, 2, 0)
+    near_product(0, 1, 1)
+    near_product(0, 1, 0)
+    to_ring(6, 2, 1)
+    near_product(1, 1, 1)
+    to_ring(6, 2, 0)
+    near_product(1, 1, 0)
+    to_ring(8, 2, 1)
     relay(0, 0)
     relay(1, 0)
-    for q in (6, 8, 7, 9):
-        to_ring(q)
-    from_ring(0)
-    from_ring(1)
+    to_ring(8, 2, 0)
     arrived("to_other", gfull.at[pl.ds(0, 4)])
 
     @pl.loop(0, 8)
@@ -337,33 +326,36 @@
 
     relay(0, 1)
     relay(1, 1)
-    for q in (2, 4, 3, 5):
-        from_ring(q)
+    for q in (2, 4):
+        for s in (1, 0):
+            from_ring(q, 2, s)
     far_product(0, 0, 1)
     far_product(0, 0, 0)
+    to_ring(10, 1, 1)
     far_product(1, 0, 1)
-    to_ring_half(10, 1)
+    to_ring(10, 1, 0)
     far_product(1, 0, 0)
-    to_ring_half(10, 0)
-    to_ring_half(11, 1)
-    to_ring_half(11, 0)
-    for q in (6, 8, 7, 9):
-        from_ring(q)
+    to_ring(11, 1, 1)
+    to_ring(11, 1, 0)
+    for q in (6, 8):
+        for s in (1, 0):
+            from_ring(q, 2, s)
     far_product(0, 1, 1)
     far_product(0, 1, 0)
-    for q in (2, 4, 6, 8):
+    for q in (2, 3, 6, 7):
         to_owner(q)
-    to_ring_half(12, 1)
+    to_ring(12, 1, 1)
     far_product(1, 1, 1)
-    to_ring_half(12, 0)
+    to_ring(12, 1, 0)
     far_product(1, 1, 0)
-    for q in (3, 5, 7, 9):
+    for q in (4, 5, 8, 9):
         to_owner(q)
-    to_ring_half(13, 1)
-    to_ring_half(13, 0)
+    to_ring(13, 1, 1)
+    to_ring(13, 1, 0)
     for q in (10, 11, 12, 13):
         for s in (1, 0):
-            from_ring_half(q, s)
+            from_ring(q, 1, s)
+            to_owner(q, lanes[s])
     arrived("owner", r3)
     totals = []
     for h in range(2):

time: 115 us -> 114 us (level)
    pallas_call x1, Pallas kernels: 113 us -> 112 us  [per_device(): pl.pallas_call(kernel, name='window_solve', out_shape=jax.ShapeDtypeStruc...]
where the time goes in v5:
time: 114 us
  Pallas kernels  112 us (98%)
  local copies, waits for them, and re-layouts  1.57 us (1%)
    pallas_call x1, Pallas kernels, per_device(): pl.pallas_call(kernel, name='window_solve', out_shape=jax.ShapeDtypeStruc...  112 us

profile of v5, /device:TPU:1, one launch (start us, length us, event | category | flops | bytes accessed | tf_op | source)
XLA Modules:
  0.0 113.7 jit_solution(14924576232061440721)
XLA Ops:
  0.0 112.1 %window_solve.1 = f32[128,256]{1,0:T(8,128)} custom-call(f32[4,4,504,256]{3,2,1,0:T(8,128)} %bitcast.1, f32[504,1024]{1,0:T(8,128)} %panel.1, f32[128,256]{1,0:T(8,128)} %rhs.1, f32[8,1024]{1,0:T(8,128)} %block.1), custom_call_target="tpu_custom_call" | custom-call | tf_op jit(solution)/shard_map/window_solve/pallas_call | solution.py:406
  112.1 1.6 %copy.6 = f32[128,256]{1,0:T(8,128)} copy(f32[128,256]{1,0:T(8,128)} %window_solve.1) | data formatting | bytes 262144

commit v6 on v5

--- a/solution.py
+++ b/solution.py
@@ -277,14 +277,20 @@
     def far_product(p, h, s):
         if s:
             arrived(("far", p, h), landing(p, 2, h))
-            turn(p, 0, 2, h, (0, 4))
+
+            @pl.loop(0, 4)
+            def _(step):
+                high, low = split(tbuf[p, SLOT[2], h, step].T)
+                tt[p, pl.ds(0, BLK), aligned(step * PART, PART, PART)] = high
+                tt[p, pl.ds(BLK, BLK), aligned(step * PART, PART, PART)] = low
+
         q = NUMBER[p, 2, h]
 
         @pl.loop(2 * s, 2 * s + 2)
         def _(step):
             at = aligned(step * 256, 256, 256)
-            value = dot(tt[p, :BLK, :], lsplit[p, :, at]) + dot(tt[p, :BLK, :DEEP], lsplit[p, DEEP:, at])
-            cbuf[q, :, at] = value
+            both = dot(tt[p, :, :DEEP], lsplit[p, DEEP:, at])
+            cbuf[q, :, at] = both[:BLK] + both[BLK:] + dot(tt[p, :BLK, :DEEP], lsplit[p, :DEEP, at])
 
         to_pair(q, 1, s)
 
@@ -332,26 +338,26 @@
     far_product(0, 0, 1)
     far_product(0, 0, 0)
     to_ring(10, 1, 1)
+    to_ring(10, 1, 0)
     far_product(1, 0, 1)
-    to_ring(10, 1, 0)
     far_product(1, 0, 0)
     to_ring(11, 1, 1)
+    far_product(0, 1, 1)
     to_ring(11, 1, 0)
-    for q in (6, 8):
-        for s in (1, 0):
-            from_ring(q, 2, s)
-    far_product(0, 1, 1)
     far_product(0, 1, 0)
-    for q in (2, 3, 6, 7):
-        to_owner(q)
     to_ring(12, 1, 1)
     far_product(1, 1, 1)
     to_ring(12, 1, 0)
     far_product(1, 1, 0)
+    to_ring(13, 1, 1)
+    for q in (6, 8):
+        for s in (1, 0):
+            from_ring(q, 2, s)
+    for q in (2, 3, 6, 7):
+        to_owner(q)
+    to_ring(13, 1, 0)
     for q in (4, 5, 8, 9):
         to_owner(q)
-    to_ring(13, 1, 1)
-    to_ring(13, 1, 0)
     for q in (10, 11, 12, 13):
         for s in (1, 0):
             from_ring(q, 1, s)

time: 114 us -> 114 us (level)
  no operation moved by 1% of the time
where the time goes in v6:
time: 114 us; the launch traced here: 113 us
  Pallas kernels  112 us (98%)
  local copies, waits for them, and re-layouts  1.57 us (1%)
    pallas_call x1, Pallas kernels, per_device(): pl.pallas_call(kernel, name='window_solve', out_shape=jax.ShapeDtypeStruc...  112 us

profile of v6, /device:TPU:1, one launch (start us, length us, event | category | flops | bytes accessed | tf_op | source)
XLA Modules:
  0.0 113.4 jit_solution(3658373588397653679)
XLA Ops:
  0.0 111.8 %window_solve.1 = f32[128,256]{1,0:T(8,128)} custom-call(f32[4,4,504,256]{3,2,1,0:T(8,128)} %bitcast.1, f32[504,1024]{1,0:T(8,128)} %panel.1, f32[128,256]{1,0:T(8,128)} %rhs.1, f32[8,1024]{1,0:T(8,128)} %block.1), custom_call_target="tpu_custom_call" | custom-call | tf_op jit(solution)/shard_map/window_solve/pallas_call | solution.py:412
  111.8 1.6 %copy.6 = f32[128,256]{1,0:T(8,128)} copy(f32[128,256]{1,0:T(8,128)} %window_solve.1) | data formatting | bytes 262144

commit v7 on v6

--- a/solution.py
+++ b/solution.py
@@ -372,6 +372,7 @@
                 total += r3[q - 2]
         totals.append(total)
 
+    own = aligned(core * 64 + x * QUARTER, QUARTER, QUARTER)
     left = -jnp.concatenate(totals, axis=0)
     for j in range(7, -1, -1):
         high, low = split(left[:, j * BLK : (j + 1) * BLK])
@@ -379,16 +380,15 @@
         both = dot(jnp.concatenate([high, low], axis=0), gsplit[0, j, :, :width])
         step = both[:32] + both[32:] + dot(high, gsplit[1, j, :, :width])
         xs[j] = step[:, j * BLK :].reshape(2, QUARTER, BLK)
+
+        @pl.when(row != j)
+        def _():
+            copy(xs.at[j], obuf.at[:, own, :], (j, col), "spread", "spread")
+
         if j:
             left = left[:, : j * BLK] - step[:, : j * BLK]
 
-    own = aligned(core * 64 + x * QUARTER, QUARTER, QUARTER)
     obuf[:, own, :] = xs[row]
-    for i in range(4):
-        for j in range(2):
-            if (i, j) != (0, 0):
-                target = where(dx=i, dc=j)
-                copy(xs.at[target[0]], obuf.at[:, own, :], target, "spread", "spread")
     arrived("spread", xs.at[pl.ds(0, 7)])
     out[...] = obuf[...].reshape(COLS, BLK).T
     gone("shards", wrow.at[0, pl.ds(0, 3)])

time: 114 us -> 113 us (level)
  no operation moved by 1% of the time
where the time goes in v7:
time: 113 us
  Pallas kernels  111 us (98%)
  local copies, waits for them, and re-layouts  1.57 us (1%)
    pallas_call x1, Pallas kernels, per_device(): pl.pallas_call(kernel, name='window_solve', out_shape=jax.ShapeDtypeStruc...  111 us

profile of v7, /device:TPU:1, one launch (start us, length us, event | category | flops | bytes accessed | tf_op | source)
XLA Modules:
  0.0 112.8 jit_solution(12299304876649005307)
XLA Ops:
  0.0 111.2 %window_solve.1 = f32[128,256]{1,0:T(8,128)} custom-call(f32[4,4,504,256]{3,2,1,0:T(8,128)} %bitcast.1, f32[504,1024]{1,0:T(8,128)} %panel.1, f32[128,256]{1,0:T(8,128)} %rhs.1, f32[8,1024]{1,0:T(8,128)} %block.1), custom_call_target="tpu_custom_call" | custom-call | tf_op jit(solution)/shard_map/window_solve/pallas_call | solution.py:412
  111.2 1.6 %copy.6 = f32[128,256]{1,0:T(8,128)} copy(f32[128,256]{1,0:T(8,128)} %window_solve.1) | data formatting | bytes 262144

commit v8 on v7

--- a/solution.py
+++ b/solution.py
@@ -18,7 +18,7 @@
 CHUNKS = [(None, 0, 0), (None, 0, 1)] + [(p, d, h) for near in ((1, 3), (2,)) for h in range(2) for p in range(2) for d in near]
 NUMBER = {chunk: q for q, chunk in enumerate(CHUNKS)}
 SLOT = (0, 1, 3, 2)
-RECEIVED, SENDING, LOCAL = 62, 15, 8
+RECEIVED, SENDING, LOCAL = 63, 15, 8
 
 
 def split(value):
@@ -256,7 +256,7 @@
 
     def to_owner(q, at=pl.ds(0, WIN)):
         p, d, _ = CHUNKS[q]
-        copy(psum.at[q, :, at], r3.at[q - 2, :, at], along(p, -d), "owner", "owner")
+        copy(psum.at[q, :, at], r3.at[q - 2, :, at], along(p, -d), ("owner", d == 2), "owner")
 
     def near_product(p, h, s):
         if s:
@@ -362,15 +362,13 @@
         for s in (1, 0):
             from_ring(q, 1, s)
             to_owner(q, lanes[s])
-    arrived("owner", r3)
-    totals = []
-    for h in range(2):
-        total = psum[h]
-        for d in (1, 3, 2):
-            for p in range(2):
-                q = NUMBER[p, d, h]
-                total += r3[q - 2]
-        totals.append(total)
+    totals = [psum[0], psum[1]]
+    for far, distances, count in ((False, (1, 3), 8), (True, (2,), 4)):
+        arrived(("owner", far), r3.at[pl.ds(8 * far, count)])
+        for h in range(2):
+            for d in distances:
+                for p in range(2):
+                    totals[h] += r3[NUMBER[p, d, h] - 2]
 
     own = aligned(core * 64 + x * QUARTER, QUARTER, QUARTER)
     left = -jnp.concatenate(totals, axis=0)

time: 113 us -> 113 us (level)
  no operation moved by 1% of the time
where the time goes in v8:
time: 113 us
  Pallas kernels  111 us (98%)
  local copies, waits for them, and re-layouts  1.57 us (1%)
    pallas_call x1, Pallas kernels, per_device(): pl.pallas_call(kernel, name='window_solve', out_shape=jax.ShapeDtypeStruc...  111 us

profile of v8, /device:TPU:1, one launch (start us, length us, event | category | flops | bytes accessed | tf_op | source)
XLA Modules:
  0.0 112.8 jit_solution(1037211975479940049)
XLA Ops:
  0.0 111.2 %window_solve.1 = f32[128,256]{1,0:T(8,128)} custom-call(f32[4,4,504,256]{3,2,1,0:T(8,128)} %bitcast.1, f32[504,1024]{1,0:T(8,128)} %panel.1, f32[128,256]{1,0:T(8,128)} %rhs.1, f32[8,1024]{1,0:T(8,128)} %block.1), custom_call_target="tpu_custom_call" | custom-call | tf_op jit(solution)/shard_map/window_solve/pallas_call | solution.py:410
  111.2 1.6 %copy.6 = f32[128,256]{1,0:T(8,128)} copy(f32[128,256]{1,0:T(8,128)} %window_solve.1) | data formatting | bytes 262144
